TPU v7x, 1024 devices: a whole 4x4x32 slice. The times are simulated.
1024 devices in a mesh: lon: 32 (over y, x, core), lat: 32 (over z).
Axes of the slice: x: 4, y: 4, z: 32, core: 2. Of those that a mesh axis runs over, the one named last changes fastest.
Arguments:
- increment: float32 [2, 137, 256, 4096], P(None, None, 'lat', 'lon'), may hold values from -6 to 6
- mixing: float32 [2, 137], replicated, may hold values from 0.02 to 0.12
- mixing_mask: int32 [256, 4096], P('lat', 'lon'), may hold values 0 or 1
- jacobian: bfloat16 [40, 20, 274], replicated, may hold values from -0.375 to 0.375
- fp_col: int32 [32, 32, 256], P('lon', 'lat'), may hold values from -1 to 1023, as said below
- fp_class: int32 [32, 32, 256], P('lon', 'lat'), may hold values from -1 to 39, as said below
- obs: float32 [32, 32, 20, 256], P('lon', 'lat'), may hold values from -6 to 6
- obs_weight: float32 [32, 32, 20, 256], P('lon', 'lat'), may hold values from 0.25 to 4
Outputs:
- gradient: float32 [2, 137, 256, 4096], P(None, None, 'lat', 'lon')
Inputs may be any that keep to these rules, and one draw needn't show every extreme that they name: `fp_col`: -1 marks an empty slot; in each group of 8 slots from one tile to one owner the live slots come first; only owners with lat index a multiple of 8 have live slots; in every draw some group is full, and some owner is full from every source tile. `fp_class`: entry [l, d, s * 8 + k] is the class of the footprint in slot [l, s, d * 8 + k] of fp_col, and -1 exactly where that slot is empty.
All inputs are finite; a program needn't handle non-finite values. No bound on the sum of `mixing_mask` on one device may be relied on, other than what follows from the above.
Results may differ from a plain program's by a relative error of at most 0.00031.
Values may be sent and summed in bfloat16 or wider, within the bound.
No kernel may reach another device: no remote copies, remote signals or barrier semaphores. Data moves between devices by JAX's collectives and lax.ppermute only.
A program may use at most 32 MiB of HBM per device.

v0:
```python
import jax
import jax.numpy as jnp
from jax import lax
from jax.sharding import PartitionSpec as P


def with_halo(x, sides, width):
    edges = {}
    for axis, dim in sides:
        count, length = (lax.axis_size(axis), x.shape[dim])
        up = [(i, (i + 1) % count) for i in range(count)]
        last = lax.slice_in_dim(x, length - width, length, axis=dim)
        first = lax.slice_in_dim(x, 0, width, axis=dim)
        edges[dim] = (
            lax.ppermute(last, axis, up),
            lax.ppermute(first, axis, [(b, a) for a, b in up]),
        )
    done = []
    for _, dim in sides:
        low, high = edges[dim]
        around = [(width, width) if d in done else (0, 0) for d in range(x.ndim)]
        x = jnp.concatenate([jnp.pad(low, around), x, jnp.pad(high, around)], axis=dim)
        done.append(dim)
    return x


def laplace(field):
    padded = with_halo(field, (("lon", 3), ("lat", 2)), 1)
    lat_index = lax.axis_index("lat")
    row_count = padded.shape[2]
    row_ids = jnp.arange(row_count, dtype=jnp.int32)
    at_edge = (row_ids == 0) & (lat_index == 0) | (row_ids == row_count - 1) & (
        lat_index == lax.axis_size("lat") - 1
    )
    padded = jnp.where(at_edge[None, None, :, None], 0.0, padded)
    vertical = padded[:, :, 2:, 1:-1] + padded[:, :, :-2, 1:-1]
    across = padded[:, :, 1:-1, 2:] + padded[:, :, 1:-1, :-2]
    return across + vertical - 4.0 * field


def class_onehot(classes, class_count):
    return (classes[None, :] == jnp.arange(class_count, dtype=jnp.int32)[:, None]).astype(
        jnp.float32
    )


def radiances(jacobian, columns, onehot):
    jac_rows = jacobian.reshape(-1, jacobian.shape[2])
    all_rows = jnp.dot(jac_rows, columns, preferred_element_type=jnp.float32)
    all_rows = all_rows.reshape(jacobian.shape[0], jacobian.shape[1], -1)
    return jnp.sum(all_rows * onehot[:, None, :], axis=0)


def adjoint_columns(jacobian, weighted, onehot):
    spread = (onehot[:, None, :] * weighted.astype(jnp.float32)[None]).astype(jnp.bfloat16)
    spread = spread.reshape(-1, spread.shape[2])
    jac_rows = jacobian.reshape(-1, jacobian.shape[2])
    return jnp.einsum("rk,rs->ks", jac_rows, spread, preferred_element_type=jnp.float32)


def departures(evolved, observed, weights, classes):
    return jnp.where(classes[None, :] >= 0, weights * (evolved - observed), 0.0).astype(
        jnp.bfloat16
    )


def on_device(increment, mixing, mixing_mask, jacobian, fp_col, fp_class, obs, obs_weight):
    column_len = 2 * increment.shape[1]
    lat_rows, lon_cells = (increment.shape[2], increment.shape[3])
    mix_scale = mixing[:, :, None, None] * mixing_mask.astype(jnp.float32)[None, None]
    advanced = increment + mix_scale * laplace(increment)
    state_cols = advanced.astype(jnp.bfloat16).reshape(column_len, lat_rows * lon_cells)
    wanted = fp_col[0, 0]
    is_live = wanted >= 0
    safe_col = jnp.maximum(wanted, 0)
    picked = jnp.where(
        is_live[None, :], jnp.take(state_cols, safe_col, axis=1), jnp.zeros((), jnp.bfloat16)
    )
    classes = fp_class[0, 0]
    observed = obs[0, 0]
    weights = obs_weight[0, 0]
    class_count = jacobian.shape[0]
    own_classes = lax.all_to_all(classes, "lat", split_axis=0, concat_axis=0, tiled=True)
    onehot = class_onehot(own_classes, class_count)
    evolved = radiances(jacobian, picked, onehot)
    arrived = lax.all_to_all(evolved, "lat", split_axis=1, concat_axis=1, tiled=True)
    weighted = departures(arrived, observed, weights, classes)
    returned = lax.all_to_all(weighted, "lat", split_axis=1, concat_axis=1, tiled=True)
    adjoint = adjoint_columns(jacobian, returned, onehot)
    summed = jnp.zeros((column_len, lat_rows * lon_cells), jnp.float32).at[:, safe_col].add(adjoint)
    summed = summed.reshape(increment.shape)
    return increment + summed + laplace(mix_scale * summed)


def solution(mesh):
    return jax.shard_map(
        on_device,
        mesh=mesh,
        in_specs=(
            P(None, None, "lat", "lon"),
            P(),
            P("lat", "lon"),
            P(),
            P("lon", "lat", None),
            P("lon", "lat", None),
            P("lon", "lat", None, None),
            P("lon", "lat", None, None),
        ),
        out_specs=P(None, None, "lat", "lon"),
        check_vma=False,
    )
```

profile of v0, /device:TPU:31, one launch (start us, length us, event | category | flops | bytes accessed | tf_op | source)
XLA Modules:
  0.0 186.0 jit_solution(3000875884529327839)
XLA Ops:
  2.5 28.4 %all-to-all-start = ((s32[32,8,1]{1,2,0:T(1,128)}), s32[32,8,1]{1,2,0:T(1,128)S(1)}, u32[]{:S(2)}, u32[]{:S(2)}) async-start(s32[32,8,1]{1,2,0:T(1,128)} %bitcast.1), calls=%async_computation | async-start | bytes 32768 | tf_op jit(solution)/shard_map/all_to_all | solution.py:83
  31.0 2.7 %fusion.29 = (f32[2,137,1,128]{3,2,1,0:T(1,128)}, f32[2,137,1,128]{3,2,1,0:T(1,128)S(1)}) fusion(f32[2,137,8,128]{3,2,1,0:T(8,128)} %param.8), kind=kLoop, calls=%fused_computation.56 | loop fusion | bytes 561152 | tf_op jit(solution)/shard_map/slice | solution.py:12
  33.7 3.1 %collective-permute-start = (f32[2,137,1,128]{3,2,1,0:T(1,128)}, f32[2,137,1,128]{3,2,1,0:T(1,128)}, u32[]{:S(2)}, u32[]{:S(2)}) collective-permute-start(f32[2,137,1,128]{3,2,1,0:T(1,128)} %get-tuple-element.13), channel_id=1, source_target_pairs={{0,1},{1,2},{2,3},{3,4},{4,5},{5,6},{6,7},{7,8},{8,9},{9,10},{10,1... | collective-permute-start | bytes 420872 | tf_op jit(solution)/shard_map/ppermute | solution.py:15
  36.8 3.4 %collective-permute-start.3 = (f32[2,137,1,128]{3,2,1,0:T(1,128)S(1)}, f32[2,137,1,128]{3,2,1,0:T(1,128)}, u32[]{:S(2)}, u32[]{:S(2)}) collective-permute-start(f32[2,137,1,128]{3,2,1,0:T(1,128)S(1)} %get-tuple-element.14), channel_id=1, source_target_pairs={{1,0},{2,1},{3,2},{4,3},{5,4},{6,5},{7,6},{8,7},{9,8},{10,9},{11,1... | collective-permute-start | bytes 420872 | tf_op jit(solution)/shard_map/ppermute | solution.py:16
  40.2 2.2 %fusion.28 = (f32[2,137,8,1]{3,2,1,0:T(8,128)S(1)}, f32[2,137,8,1]{3,2,1,0:T(8,128)S(1)}) fusion(f32[2,137,8,128]{3,2,1,0:T(8,128)} %param.8), kind=kLoop, calls=%fused_computation.55 | loop fusion | bytes 35072 | tf_op jit(solution)/shard_map/slice | solution.py:12
  43.0 3.4 %collective-permute-start.2 = (f32[2,137,8,1]{1,2,3,0:T(8,128)S(1)}, f32[2,137,8,1]{1,2,3,0:T(8,128)}, u32[]{:S(2)}, u32[]{:S(2)}) collective-permute-start(f32[2,137,8,1]{1,2,3,0:T(8,128)S(1)} %copy.43), channel_id=1, source_target_pairs={{32,0},{64,32},{96,64},{128,96},{160,128},{192,160},{224,192},{256... | collective-permute-start | bytes 26312 | tf_op jit(solution)/shard_map/ppermute | solution.py:16
  47.1 5.5 %collective-permute-start.1 = (f32[2,137,8,1]{1,2,3,0:T(8,128)S(1)}, f32[2,137,8,1]{1,2,3,0:T(8,128)S(1)}, u32[]{:S(2)}, u32[]{:S(2)}) collective-permute-start(f32[2,137,8,1]{1,2,3,0:T(8,128)S(1)} %copy.42), channel_id=1, source_target_pairs={{0,32},{32,64},{64,96},{96,128},{128,160},{160,192},{192,224},{224... | collective-permute-start | bytes 26312 | tf_op jit(solution)/shard_map/ppermute | solution.py:15
  58.1 4.3 %fusion.1 = f32[2,137,10,130]{3,2,1,0:T(8,128)S(1)} fusion(f32[2,137,1,128]{3,2,1,0:T(1,128)} %collective-permute-done.3, f32[2,137,1,128]{3,2,1,0:T(1,128)} %collective-permute-done, f32[2,137,8,1]{3,2,1,0:T(8,128)S(1)} %copy.27, f32[2,137,8,128]{3,2,1,0:T(8,128)S(1)} %copy-done, f32[2,137,8,1]{3,2,1,0:T(8,128)S(1)} %copy.26, pred[10]{0:T(512)(128)(4,1)S(1)} %and_or_fusion), kind=kLoop, calls=%fused_computation.6 | loop fusion | flops 3205800 | bytes 2845226 | tf_op jit(solution)/shard_map/jit(_where)/select_n | solution.py:35
  68.4 21.2 %all-to-all-start.1 = ((f32[32,1,160]{2,1,0:T(1,128)}), f32[32,1,160]{2,1,0:T(1,128)S(1)}, u32[]{:S(2)}, u32[]{:S(2)}) async-start(f32[32,1,160]{2,1,0:T(1,128)} %reshape.151), calls=%async_computation.1 | async-start | bytes 65536 | tf_op jit(solution)/shard_map/all_to_all | solution.py:86
  90.0 21.6 %all-to-all-done.1 = f32[32,1,160]{2,1,0:T(1,128)S(1)} async-done(((f32[32,1,160]{2,1,0:T(1,128)}), f32[32,1,160]{2,1,0:T(1,128)S(1)}, u32[]{:S(2)}, u32[]{:S(2)}) %all-to-all-start.1) | async-done | bytes 20512 | tf_op jit(solution)/shard_map/all_to_all | solution.py:86
  113.1 28.3 %all_to_all.24 = bf16[20,32,8]{0,2,1:T(8,128)(2,1)S(1)} all-to-all(bf16[20,32,8]{0,2,1:T(8,128)(2,1)S(1)} %fusion.19), channel_id=1, replica_groups=mesh['lon'=32,'lat'=32] {'lat'}, dimensions={1} | all-to-all | bytes 20480 | tf_op jit(solution)/shard_map/all_to_all | solution.py:88
  141.9 2.8 %scatter_custom_fusion = f32[274,1024]{0,1:T(8,128)S(1)} fusion(s32[256]{0:T(256)S(1)} %bitcast.43, f32[256,274]{1,0:T(8,128)S(1)} %convolution_bitcast_fusion.1, f32[]{:T(128)} %constant.10.clone.1), kind=kCustom, calls=%fused_computation.27 | custom fusion | flops 70144 | bytes 1122308 | tf_op jit(solution)/shard_map/scatter-add | solution.py:90
  149.0 2.2 %collective-permute-start.4 = (f32[2,137,1,128]{3,2,1,0:T(1,128)}, f32[2,137,1,128]{3,2,1,0:T(1,128)}, u32[]{:S(2)}, u32[]{:S(2)}) collective-permute-start(f32[2,137,1,128]{3,2,1,0:T(1,128)} %get-tuple-element.9), channel_id=1, source_target_pairs={{0,1},{1,2},{2,3},{3,4},{4,5},{5,6},{6,7},{7,8},{8,9},{9,10},{10,1... | collective-permute-start | bytes 420872 | tf_op jit(solution)/shard_map/ppermute | solution.py:15
  151.2 4.3 %collective-permute-start.7 = (f32[2,137,1,128]{3,2,1,0:T(1,128)S(1)}, f32[2,137,1,128]{3,2,1,0:T(1,128)}, u32[]{:S(2)}, u32[]{:S(2)}) collective-permute-start(f32[2,137,1,128]{3,2,1,0:T(1,128)S(1)} %get-tuple-element.10), channel_id=1, source_target_pairs={{1,0},{2,1},{3,2},{4,3},{5,4},{6,5},{7,6},{8,7},{9,8},{10,9},{11,1... | collective-permute-start | bytes 420872 | tf_op jit(solution)/shard_map/ppermute | solution.py:16
  155.5 1.7 fusion.26
  157.2 1.9 %copy.36 = f32[2,137,8,1]{1,2,3,0:T(8,128)S(1)} copy(f32[2,137,8,1]{3,2,1,0:T(8,128)} %get-tuple-element.7) | data formatting | bytes 17536 | tf_op jit(solution)/shard_map/slice | solution.py:12
  159.0 6.2 %collective-permute-start.5 = (f32[2,137,8,1]{1,2,3,0:T(8,128)S(1)}, f32[2,137,8,1]{1,2,3,0:T(8,128)}, u32[]{:S(2)}, u32[]{:S(2)}) collective-permute-start(f32[2,137,8,1]{1,2,3,0:T(8,128)S(1)} %copy.36), channel_id=1, source_target_pairs={{0,32},{32,64},{64,96},{96,128},{128,160},{160,192},{192,224},{224... | collective-permute-start | bytes 26312 | tf_op jit(solution)/shard_map/ppermute | solution.py:15
  165.3 2.5 %copy.37 = f32[2,137,8,1]{1,2,3,0:T(8,128)} copy(f32[2,137,8,1]{3,2,1,0:T(8,128)} %get-tuple-element.8) | data formatting | bytes 17536 | tf_op jit(solution)/shard_map/slice | solution.py:13
  167.8 2.0 %collective-permute-start.6 = (f32[2,137,8,1]{1,2,3,0:T(8,128)}, f32[2,137,8,1]{1,2,3,0:T(8,128)}, u32[]{:S(2)}, u32[]{:S(2)}) collective-permute-start(f32[2,137,8,1]{1,2,3,0:T(8,128)} %copy.37), channel_id=1, source_target_pairs={{32,0},{64,32},{96,64},{128,96},{160,128},{192,160},{224,192},{256... | collective-permute-start | bytes 26312 | tf_op jit(solution)/shard_map/ppermute | solution.py:16
  169.8 2.4 %copy.38 = f32[2,137,8,1]{3,2,1,0:T(8,128)} copy(f32[2,137,8,1]{1,2,3,0:T(8,128)} %collective-permute-done.5) | data formatting | bytes 17536 | tf_op jit(solution)/shard_map/ppermute | solution.py:15
  172.2 4.4 %collective-permute-done.6 = f32[2,137,8,1]{1,2,3,0:T(8,128)} collective-permute-done((f32[2,137,8,1]{1,2,3,0:T(8,128)}, f32[2,137,8,1]{1,2,3,0:T(8,128)}, u32[]{:S(2)}, u32[]{:S(2)}) %collective-permute-start.6) | collective-permute-done | bytes 8800 | tf_op jit(solution)/shard_map/ppermute | solution.py:16
  176.6 2.4 %copy.39 = f32[2,137,8,1]{3,2,1,0:T(8,128)} copy(f32[2,137,8,1]{1,2,3,0:T(8,128)} %collective-permute-done.6) | data formatting | bytes 17536 | tf_op jit(solution)/shard_map/ppermute | solution.py:16
  179.0 4.7 %fusion = f32[2,137,10,130]{3,2,1,0:T(8,128)S(1)} fusion(f32[2,137,1,128]{3,2,1,0:T(1,128)} %collective-permute-done.7, f32[2,137,1,128]{3,2,1,0:T(1,128)} %collective-permute-done.4, f32[2,137,8,1]{3,2,1,0:T(8,128)} %copy.39, f32[2,137,8,128]{3,2,1,0:T(8,128)S(1)} %multiply_multiply_fusion, f32[2,137,8,1]{3,2,1,0:T(8,128)} %copy.38, ...), kind=kLoop, calls=%fused_computation.3 | loop fusion | flops 3205800 | bytes 2845226 | tf_op jit(solution)/shard_map/jit(_where)/select_n | solution.py:35
  183.7 2.3 %fusion.6 = f32[2,137,8,128]{3,2,1,0:T(8,128)} fusion(f32[2,137,10,130]{3,2,1,0:T(8,128)S(1)} %fusion, f32[2,137,8,128]{3,2,1,0:T(8,128)S(1)} %copy-done, f32[2,137,8,128]{3,2,1,0:T(8,128)S(1)} %bitcast.36, f32[8,128]{1,0:T(8,128)S(1)} %convert_element_type.36, f32[2,137]{1,0:T(2,128)S(1)} %copy-done.7), kind=kLoop, calls=%fused_computation.19 | loop fusion | flops 2525184 | bytes 7861320 | tf_op jit(solution)/shard_map/add | solution.py:92
  (78 shorter events, 21.6 us)
Async XLA Ops:
  2.5 52.0 %all-to-all-start = ((s32[32,8,1]{1,2,0:T(1,128)}), s32[32,8,1]{1,2,0:T(1,128)S(1)}, u32[]{:S(2)}, u32[]{:S(2)}) async-start(s32[32,8,1]{1,2,0:T(1,128)} %bitcast.1), calls=%async_computation | async-start | bytes 32768 | tf_op jit(solution)/shard_map/all_to_all | solution.py:83
  33.7 24.4 %collective-permute-start = (f32[2,137,1,128]{3,2,1,0:T(1,128)}, f32[2,137,1,128]{3,2,1,0:T(1,128)}, u32[]{:S(2)}, u32[]{:S(2)}) collective-permute-start(f32[2,137,1,128]{3,2,1,0:T(1,128)} %get-tuple-element.13), channel_id=1, source_target_pairs={{0,1},{1,2},{2,3},{3,4},{4,5},{5,6},{6,7},{7,8},{8,9},{9,10},{10,1... | collective-permute-start | bytes 420872 | tf_op jit(solution)/shard_map/ppermute | solution.py:15
  36.8 21.2 %collective-permute-start.3 = (f32[2,137,1,128]{3,2,1,0:T(1,128)S(1)}, f32[2,137,1,128]{3,2,1,0:T(1,128)}, u32[]{:S(2)}, u32[]{:S(2)}) collective-permute-start(f32[2,137,1,128]{3,2,1,0:T(1,128)S(1)} %get-tuple-element.14), channel_id=1, source_target_pairs={{1,0},{2,1},{3,2},{4,3},{5,4},{6,5},{7,6},{8,7},{9,8},{10,9},{11,1... | collective-permute-start | bytes 420872 | tf_op jit(solution)/shard_map/ppermute | solution.py:16
  42.4 10.2 %copy-start.9 = (s32[1,1,256]{2,1,0:T(1,128)S(1)}, s32[1,1,256]{2,1,0:T(1,128)}, u32[]{:S(2)}) copy-start(s32[1,1,256]{2,1,0:T(1,128)} %param.12) | copy-start | bytes 3076
  42.4 10.9 %copy-start.8 = (s32[8,128]{1,0:T(8,128)S(1)}, s32[8,128]{1,0:T(8,128)}, u32[]{:S(2)}) copy-start(s32[8,128]{1,0:T(8,128)} %param.10) | copy-start | bytes 12292
  42.4 10.9 %copy-start.2 = (bf16[40,20,274]{2,0,1:T(8,128)(2,1)S(1)}, bf16[40,20,274]{2,0,1:T(8,128)(2,1)}, u32[]{:S(2)}) copy-start(bf16[40,20,274]{2,0,1:T(8,128)(2,1)} %param.11) | copy-start | bytes 1315204
  43.0 13.6 %collective-permute-start.2 = (f32[2,137,8,1]{1,2,3,0:T(8,128)S(1)}, f32[2,137,8,1]{1,2,3,0:T(8,128)}, u32[]{:S(2)}, u32[]{:S(2)}) collective-permute-start(f32[2,137,8,1]{1,2,3,0:T(8,128)S(1)} %copy.43), channel_id=1, source_target_pairs={{32,0},{64,32},{96,64},{128,96},{160,128},{192,160},{224,192},{256... | collective-permute-start | bytes 26312 | tf_op jit(solution)/shard_map/ppermute | solution.py:16
  47.1 8.8 %collective-permute-start.1 = (f32[2,137,8,1]{1,2,3,0:T(8,128)S(1)}, f32[2,137,8,1]{1,2,3,0:T(8,128)S(1)}, u32[]{:S(2)}, u32[]{:S(2)}) collective-permute-start(f32[2,137,8,1]{1,2,3,0:T(8,128)S(1)} %copy.42), channel_id=1, source_target_pairs={{0,32},{32,64},{64,96},{96,128},{128,160},{160,192},{192,224},{224... | collective-permute-start | bytes 26312 | tf_op jit(solution)/shard_map/ppermute | solution.py:15
  53.3 4.8 %copy-start.10 = (pred[10]{0:T(512)(128)(4,1)}, pred[10]{0:T(512)(128)(4,1)S(1)}, u32[]{:S(2)}) copy-start(pred[10]{0:T(512)(128)(4,1)S(1)} %and_or_fusion) | copy-start | bytes 34
  55.9 2.2 %copy-start = (f32[2,137,8,128]{3,2,1,0:T(8,128)S(1)}, f32[2,137,8,128]{3,2,1,0:T(8,128)}, u32[]{:S(2)}) copy-start(f32[2,137,8,128]{3,2,1,0:T(8,128)} %param.8) | copy-start | bytes 3366916
  58.0 4.4 %copy-start.7 = (f32[2,137]{1,0:T(2,128)S(1)}, f32[2,137]{1,0:T(2,128)}, u32[]{:S(2)}) copy-start(f32[2,137]{1,0:T(2,128)} %param.9) | copy-start | bytes 3292
  63.8 1.5 copy-start.1
  66.5 0.8 copy-start.4
  67.3 22.3 %copy-start.12 = (s32[1,1,256]{2,1,0:T(1,128)S(1)}, s32[1,1,256]{2,1,0:T(1,128)}, u32[]{:S(2)}) copy-start(s32[1,1,256]{2,1,0:T(1,128)} %param.13) | copy-start | bytes 3076
  67.3 22.4 %copy-start.5 = (f32[1,1,20,256]{3,1,2,0:T(1,128)S(1)}, f32[1,1,20,256]{3,1,2,0:T(1,128)}, u32[]{:S(2)}) copy-start(f32[1,1,20,256]{3,1,2,0:T(1,128)} %param.14) | copy-start | bytes 61444
  67.3 22.5 %copy-start.6 = (f32[1,1,20,256]{3,1,2,0:T(1,128)S(1)}, f32[1,1,20,256]{3,1,2,0:T(1,128)}, u32[]{:S(2)}) copy-start(f32[1,1,20,256]{3,1,2,0:T(1,128)} %param.15) | copy-start | bytes 61444
  67.5 74.0 %copy-start.3 = (bf16[40,20,274]{2,0,1:T(8,128)(2,1)S(1)}, bf16[40,20,274]{2,0,1:T(8,128)(2,1)}, u32[]{:S(2)}) copy-start(bf16[40,20,274]{2,0,1:T(8,128)(2,1)} %param.11) | copy-start | bytes 1315204
  68.4 43.2 %all-to-all-start.1 = ((f32[32,1,160]{2,1,0:T(1,128)}), f32[32,1,160]{2,1,0:T(1,128)S(1)}, u32[]{:S(2)}, u32[]{:S(2)}) async-start(f32[32,1,160]{2,1,0:T(1,128)} %reshape.151), calls=%async_computation.1 | async-start | bytes 65536 | tf_op jit(solution)/shard_map/all_to_all | solution.py:86
  149.0 30.0 %collective-permute-start.4 = (f32[2,137,1,128]{3,2,1,0:T(1,128)}, f32[2,137,1,128]{3,2,1,0:T(1,128)}, u32[]{:S(2)}, u32[]{:S(2)}) collective-permute-start(f32[2,137,1,128]{3,2,1,0:T(1,128)} %get-tuple-element.9), channel_id=1, source_target_pairs={{0,1},{1,2},{2,3},{3,4},{4,5},{5,6},{6,7},{7,8},{8,9},{9,10},{10,1... | collective-permute-start | bytes 420872 | tf_op jit(solution)/shard_map/ppermute | solution.py:15
  151.2 27.7 %collective-permute-start.7 = (f32[2,137,1,128]{3,2,1,0:T(1,128)S(1)}, f32[2,137,1,128]{3,2,1,0:T(1,128)}, u32[]{:S(2)}, u32[]{:S(2)}) collective-permute-start(f32[2,137,1,128]{3,2,1,0:T(1,128)S(1)} %get-tuple-element.10), channel_id=1, source_target_pairs={{1,0},{2,1},{3,2},{4,3},{5,4},{6,5},{7,6},{8,7},{9,8},{10,9},{11,1... | collective-permute-start | bytes 420872 | tf_op jit(solution)/shard_map/ppermute | solution.py:16
  159.0 10.8 %collective-permute-start.5 = (f32[2,137,8,1]{1,2,3,0:T(8,128)S(1)}, f32[2,137,8,1]{1,2,3,0:T(8,128)}, u32[]{:S(2)}, u32[]{:S(2)}) collective-permute-start(f32[2,137,8,1]{1,2,3,0:T(8,128)S(1)} %copy.36), channel_id=1, source_target_pairs={{0,32},{32,64},{64,96},{96,128},{128,160},{160,192},{192,224},{224... | collective-permute-start | bytes 26312 | tf_op jit(solution)/shard_map/ppermute | solution.py:15
  167.8 11.2 %copy-start.11 = (pred[10]{0:T(512)(128)(4,1)S(1)}, pred[10]{0:T(512)(128)(4,1)}, u32[]{:S(2)}) copy-start(pred[10]{0:T(512)(128)(4,1)} %copy-done.10) | copy-start | bytes 34
  167.8 8.8 %collective-permute-start.6 = (f32[2,137,8,1]{1,2,3,0:T(8,128)}, f32[2,137,8,1]{1,2,3,0:T(8,128)}, u32[]{:S(2)}, u32[]{:S(2)}) collective-permute-start(f32[2,137,8,1]{1,2,3,0:T(8,128)} %copy.37), channel_id=1, source_target_pairs={{32,0},{64,32},{96,64},{128,96},{160,128},{192,160},{224,192},{256... | collective-permute-start | bytes 26312 | tf_op jit(solution)/shard_map/ppermute | solution.py:16
where the time goes:
time: 187 us; the launch traced here: 186 us
  starting transfers between devices  79.8 us (43%)
  local copies, waits for them, and re-layouts  29.8 us (16%)
  blocking collectives  28.3 us (15%)
  waiting for transfers between devices  26 us (14%)
  other arithmetic  20 us (11%)
    all_to_all x1, starting transfers between devices, on_device(): lax.all_to_all(classes, 'lat', split_axis=0, concat_axis=0, tiled=True)  28.4 us
    all_to_all x1, blocking collectives, on_device(): lax.all_to_all(weighted, 'lat', split_axis=1, concat_axis=1, tiled=True)  28.3 us
    all_to_all x1, waiting for transfers between devices, on_device(): lax.all_to_all(evolved, 'lat', split_axis=1, concat_axis=1, tiled=True)  21.6 us
    all_to_all x1, starting transfers between devices, on_device(): lax.all_to_all(evolved, 'lat', split_axis=1, concat_axis=1, tiled=True)  21.2 us
    ppermute x4, starting transfers between devices, with_halo(): lax.ppermute(last, axis, up)  17.1 us
    ppermute x4, starting transfers between devices, with_halo(): lax.ppermute(first, axis, [(b, a) for a, b in up])  13.1 us
    slice x5, local copies, waits for them, and re-layouts, with_halo(): last = lax.slice_in_dim(x, length - width, length, axis=dim)  9.28 us
    select_n x2, other arithmetic, laplace(): padded = jnp.where(at_edge[None, None, :, None], 0.0, padded)  9.02 us
  transfers between devices with their start and end apart: 10, of which 2 were waited for; matrix products, arithmetic and copies ran while one was open for 12% of the time, Pallas kernels for 0%

commit v1 on v0

v1 whole, which is shorter than its diff:
```python
import jax
import jax.numpy as jnp
from jax import lax
from jax.experimental import pallas as pl
from jax.experimental.pallas import tpu as pltpu
from jax.sharding import PartitionSpec as P

OWN_EVERY = 8
SLOT = 8
ROWS = 8
LANES = 128
STRIDE = 48
CH = 20
NOWHERE = -1000000


def iota(shape, dim):
    return lax.broadcasted_iota(jnp.int32, shape, dim)


def call(body, out_shape, scratch=(), flops=1000000):
    return pl.pallas_call(
        body,
        out_shape=out_shape,
        scratch_shapes=list(scratch),
        cost_estimate=pl.CostEstimate(flops=flops, bytes_accessed=1000000, transcendentals=0),
    )


def record_spots():
    return [((k * STRIDE) // LANES, (k * STRIDE) % LANES) for k in range(SLOT)]


def records_body(obs_ref, weight_ref, class_ref, out_ref, wide_ref, tall_ref, flat_ref):
    peers = out_ref.shape[0]
    wide_ref[...] = jnp.zeros(wide_ref.shape, jnp.float32)
    for ch in range(CH):
        wide_ref[ch : ch + 1, :] = obs_ref[ch]
        wide_ref[24 + ch : 25 + ch, :] = weight_ref[ch]
    wide_ref[CH : CH + 1, :] = class_ref[0].astype(jnp.float32)
    tall_ref[...] = jnp.transpose(wide_ref[...])
    lane = iota((peers, LANES), 1)
    tiles = [jnp.zeros((peers, LANES), jnp.float32) for _ in range(SLOT * STRIDE // LANES)]
    for k, (tile, off) in enumerate(record_spots()):
        part = tall_ref[pl.ds(k, peers, stride=SLOT), :]
        part = pltpu.roll(part, off, 1) if off else part
        if off + STRIDE <= LANES:
            tiles[tile] = tiles[tile] + part
        else:
            tiles[tile] = tiles[tile] + jnp.where(lane >= off, part, 0.0)
            tiles[tile + 1] = tiles[tile + 1] + jnp.where(lane < off, part, 0.0)
    for i, value in enumerate(tiles):
        flat_ref[:, i * LANES : (i + 1) * LANES] = value
    for s in range(peers):
        out_ref[s] = flat_ref[s : s + 1, :]


def edges_body(inc_ref, first_ref, last_ref, right_ref, left_ref):
    depth = first_ref.shape[0]
    lane = iota((depth, LANES), 1)
    right = jnp.zeros((depth, LANES), jnp.float32)
    left = jnp.zeros((depth, LANES), jnp.float32)
    for r in range(ROWS):
        row = inc_ref[pl.ds(r, depth, stride=ROWS), :]
        if r == 0:
            first_ref[...] = row
        if r == ROWS - 1:
            last_ref[...] = row
        right = jnp.where(lane == r, pltpu.roll(row, r + 1, 1), right)
        left = jnp.where(lane == ROWS + r, pltpu.roll(row, ROWS + r, 1), left)
    right_ref[...] = right
    left_ref[...] = left


def state_body(inc_ref, up_ref, down_ref, from_left_ref, from_right_ref, col_ref, mask_ref,
               mix_ref, jac_ref, seen_ref, meta_ref):
    depth = up_ref.shape[0]
    lane8 = iota((8, LANES), 1)
    cols = jnp.full((8, LANES), NOWHERE, jnp.int32)
    owners = col_ref.shape[1] // (SLOT * OWN_EVERY)
    for g in range(owners):
        start = g * SLOT * OWN_EVERY
        tile = jnp.broadcast_to(col_ref[:, start // LANES * LANES : start // LANES * LANES + LANES], (8, LANES))
        shift = (g * SLOT - start % LANES) % LANES
        tile = pltpu.roll(tile, shift, 1) if shift else tile
        cols = jnp.where((lane8 >= g * SLOT) & (lane8 < (g + 1) * SLOT), tile, cols)
    cols = jnp.where(cols >= 0, cols, NOWHERE)
    both = jnp.where(lane8 < 32, cols, jnp.where(lane8 < 64, pltpu.roll(cols, 32, 1), NOWHERE))
    want = jnp.broadcast_to(both[0:1, :], (LANES, LANES))
    sub = iota((LANES, LANES), 0)
    plain = iota((LANES, LANES), 1) < 32

    def split_dot(x, chosen):
        high = x.astype(jnp.bfloat16)
        low = (x - high.astype(jnp.float32)).astype(jnp.bfloat16)
        return jnp.dot(
            jnp.concatenate([high, low], 1), jnp.concatenate([chosen, chosen], 0),
            preferred_element_type=jnp.float32,
        )

    total = jnp.zeros((depth, LANES), jnp.float32)
    masked = jnp.zeros((8, LANES), jnp.float32)
    for r in range(ROWS):
        point = sub + r * LANES
        here = jnp.where(want == point, 1.0, 0.0)
        beside = jnp.where((want == point - 1) & (sub != 0), 1.0, 0.0)
        beside = beside + jnp.where((want == point + 1) & (sub != LANES - 1), 1.0, 0.0)
        beside = beside + jnp.where((want == point - LANES) | (want == point + LANES), 1.0, 0.0)
        chosen = jnp.where(plain, here, beside - 4.0 * here).astype(jnp.bfloat16)
        total = total + split_dot(inc_ref[pl.ds(r, depth, stride=ROWS), :], chosen)
        mask_row = jnp.broadcast_to(mask_ref[r : r + 1, :].astype(jnp.bfloat16), (8, LANES))
        masked = masked + jnp.dot(mask_row, chosen, preferred_element_type=jnp.float32)
    near = ~plain
    chosen = jnp.where(near & (want == sub), 1.0, 0.0).astype(jnp.bfloat16)
    total = total + split_dot(up_ref[...], chosen)
    chosen = jnp.where(near & (want == sub + (ROWS - 1) * LANES), 1.0, 0.0).astype(jnp.bfloat16)
    total = total + split_dot(down_ref[...], chosen)
    on_left = (sub < ROWS) & (want == sub * LANES)
    on_right = (sub >= ROWS) & (sub < 2 * ROWS) & (want == (sub - ROWS) * LANES + LANES - 1)
    chosen = jnp.where(near & (on_left | on_right), 1.0, 0.0).astype(jnp.bfloat16)
    total = total + split_dot(from_left_ref[...] + from_right_ref[...], chosen)

    state = total + mix_ref[...] * masked[0:1, :] * pltpu.roll(total, LANES - 32, 1)
    state = jnp.where(iota((depth, LANES), 1) < 32, state, 0.0).astype(jnp.bfloat16)
    seen_ref[...] = jnp.dot(jac_ref[...], state, preferred_element_type=jnp.float32)
    meta_ref[0:1, :] = cols[0:1, :].astype(jnp.float32)
    meta_ref[1:2, :] = masked[0:1, :]
    meta_ref[2:8, :] = jnp.zeros((6, LANES), jnp.float32)


def departures_body(records_ref, seen_ref, meta_ref, out_ref, row_ref, spot_ref):
    owners = records_ref.shape[0] // OWN_EVERY
    classes = seen_ref.shape[0] // CH
    row_ref[...] = jnp.zeros(row_ref.shape, jnp.float32)
    spot_ref[...] = jnp.zeros(spot_ref.shape, jnp.float32)
    for g in range(owners):
        row_ref[g : g + 1, :] = records_ref[g * OWN_EVERY]
    lane8 = iota((8, LANES), 1)
    tiles = [row_ref[:, i * LANES : (i + 1) * LANES] for i in range(SLOT * STRIDE // LANES)]
    for k, (tile, off) in enumerate(record_spots()):
        part = pltpu.roll(tiles[tile], LANES - off, 1) if off else tiles[tile]
        if off + STRIDE > LANES:
            part = jnp.where(lane8 < LANES - off, part, pltpu.roll(tiles[tile + 1], LANES - off, 1))
        for g in range(owners):
            spot_ref[g * SLOT + k : g * SLOT + k + 1, :] = part[g : g + 1, :]
    turned = jnp.transpose(spot_ref[...])
    lane1 = iota((1, LANES), 1)
    kind = jnp.where(lane1 < owners * SLOT, turned[CH : CH + 1, :], -1.0)
    chosen = jnp.broadcast_to(kind, (classes, LANES)).astype(jnp.int32) == iota((classes, LANES), 0)
    out_ref[...] = jnp.zeros(out_ref.shape, jnp.float32)
    for ch in range(CH):
        rows = seen_ref[ch * classes : (ch + 1) * classes, :]
        out_ref[ch : ch + 1, :] = jnp.sum(jnp.where(chosen, rows, 0.0), axis=0, keepdims=True)
    evolved = out_ref[0:CH, :]
    weighted = turned[24 : 24 + CH, :] * (evolved - turned[0:CH, :])
    weighted = jnp.where(jnp.broadcast_to(kind, (CH, LANES)) >= 0, weighted, 0.0)
    out_ref[0:CH, :] = weighted.astype(jnp.bfloat16).astype(jnp.float32)
    live = lane1 < owners * SLOT
    out_ref[CH : CH + 1, :] = jnp.where(live, kind, 0.0)
    out_ref[CH + 1 : CH + 2, :] = jnp.where(live, meta_ref[0:1, :], 0.0)
    out_ref[CH + 2 : CH + 3, :] = jnp.where(live, meta_ref[1:2, :], 0.0)


def gradient_body(own_ref, left_ref, right_ref, up_ref, down_ref, turned_jac_ref, mix_ref, inc_ref,
                  out_ref, spread_ref, flip_ref):
    depth = turned_jac_ref.shape[0]
    classes = turned_jac_ref.shape[1] // CH
    four = own_ref[...] + pltpu.roll(left_ref[...], 32, 1) + pltpu.roll(right_ref[...], 64, 1)
    four = four + pltpu.roll(up_ref[...], 96, 1)
    both = jnp.concatenate([four, down_ref[...]], 1)
    kinds = jnp.broadcast_to(both[CH : CH + 1, :], (classes, 2 * LANES)).astype(jnp.int32)
    chosen = kinds == iota((classes, 2 * LANES), 0)
    for ch in range(CH):
        spread_ref[ch * classes : (ch + 1) * classes, :] = jnp.where(chosen, both[ch : ch + 1, :], 0.0)
    adjoint = jnp.dot(turned_jac_ref[...], spread_ref[...].astype(jnp.bfloat16), preferred_element_type=jnp.float32)

    lane = iota((depth, LANES), 1)
    own = jnp.where(lane < 32, adjoint[:, 0:LANES], 0.0)
    own_high = own.astype(jnp.bfloat16).astype(jnp.float32)
    rest = own - own_high
    own_mid = rest.astype(jnp.bfloat16).astype(jnp.float32)
    own_low = rest - own_mid
    summed = own_high + pltpu.roll(own_mid, 32, 1) + pltpu.roll(own_low, 64, 1)
    mixed = mix_ref[...] * adjoint
    mixed_high = mixed.astype(jnp.bfloat16).astype(jnp.float32)
    mixed_low = mixed - mixed_high
    last = jnp.where(lane < 32, mixed_high[:, LANES:], 0.0)
    last = last + pltpu.roll(jnp.where(lane < 32, mixed_low[:, LANES:], 0.0), 32, 1)
    left_side = jnp.concatenate(
        [summed, mixed_high[:, 0:LANES], mixed_low[:, 0:LANES], last], 1
    ).astype(jnp.bfloat16)

    flip_ref[...] = jnp.zeros(flip_ref.shape, jnp.float32)
    lane1 = iota((1, LANES), 1)
    own_col = own_ref[CH + 1 : CH + 2, :]
    thrice = own_col + pltpu.roll(jnp.broadcast_to(own_col, (8, LANES)), 32, 1)[0:1, :]
    thrice = thrice + pltpu.roll(jnp.broadcast_to(own_col, (8, LANES)), 64, 1)[0:1, :]
    flip_ref[0:1, :] = jnp.where(lane1 < 96, thrice, float(NOWHERE))
    flip_ref[1:2, :] = four[CH + 1 : CH + 2, :]
    flip_ref[2:3, :] = four[CH + 2 : CH + 3, :]
    down_col = jnp.broadcast_to(down_ref[CH + 1 : CH + 2, :], (8, LANES))
    down_on = jnp.broadcast_to(down_ref[CH + 2 : CH + 3, :], (8, LANES))
    flip_ref[3:4, :] = (down_col + pltpu.roll(down_col, 32, 1))[0:1, :]
    flip_ref[4:5, :] = (down_on + pltpu.roll(down_on, 32, 1))[0:1, :]
    flipped = jnp.transpose(flip_ref[...])
    col3 = jnp.broadcast_to(flipped[:, 0:1], (LANES, LANES)).astype(jnp.int32)
    col = jnp.broadcast_to(flipped[:, 1:2], (LANES, LANES)).astype(jnp.int32)
    on = jnp.broadcast_to(flipped[:, 2:3], (LANES, LANES))
    col_down = jnp.broadcast_to(flipped[:, 3:4], (LANES, LANES)).astype(jnp.int32)
    on_down = jnp.broadcast_to(flipped[:, 4:5], (LANES, LANES))
    across = iota((LANES, LANES), 1)
    spot = iota((32, LANES), 1)
    none = jnp.zeros((32, LANES), jnp.float32)

    def right_side(r):
        point = across + r * LANES
        pick = jnp.where(col3 == point, 1.0, 0.0)
        mine, lefts, rights, ups = (col[32 * i : 32 * (i + 1), :] for i in range(4))
        here = spot + r * LANES
        stencil = jnp.where(mine == here, -4.0, 0.0)
        stencil = stencil + jnp.where((mine == here - 1) & (spot != 0), 1.0, 0.0)
        stencil = stencil + jnp.where((mine == here + 1) & (spot != LANES - 1), 1.0, 0.0)
        stencil = stencil + jnp.where((mine == here - LANES) | (mine == here + LANES), 1.0, 0.0)
        to_left = jnp.where((spot == 0) & (lefts == r * LANES + LANES - 1), 1.0, 0.0)
        to_right = jnp.where((spot == LANES - 1) & (rights == r * LANES), 1.0, 0.0)
        to_up = jnp.where(ups == spot + (ROWS - 1) * LANES, 1.0, 0.0) if r == 0 else none
        reach = jnp.concatenate([stencil, to_left, to_right, to_up], 0) * on
        if r == ROWS - 1:
            to_down = jnp.where(col_down == across, 1.0, 0.0) * on_down
        else:
            to_down = jnp.zeros((LANES, LANES), jnp.float32)
        return jnp.concatenate([pick, reach, reach, to_down], 0).astype(jnp.bfloat16)

    for r in range(0, ROWS, 2):
        pair = jnp.concatenate([right_side(r), right_side(r + 1)], 1)
        added = jnp.dot(left_side, pair, preferred_element_type=jnp.float32)
        for i in range(2):
            rows = pl.ds(r + i, depth, stride=ROWS)
            out_ref[rows, :] = inc_ref[rows, :] + added[:, i * LANES : (i + 1) * LANES]


def moved(x, axis, step, periodic):
    count = lax.axis_size(axis)
    pairs = [(i, (i + step) % count) for i in range(count) if periodic or 0 <= i + step < count]
    return lax.ppermute(x, axis, pairs)


def on_device(increment, mixing, mixing_mask, jacobian, fp_col, fp_class, obs, obs_weight):
    f32 = jnp.float32
    peers = lax.axis_size("lat")
    depth = 2 * increment.shape[1]
    slots = fp_col.shape[2]
    kinds = jacobian.shape[0] * CH
    inc = increment.reshape(depth * ROWS, LANES)
    mix = mixing.reshape(depth, 1)
    jac = jnp.transpose(jacobian, (1, 0, 2)).reshape(kinds, depth)
    turned_jac = jnp.transpose(jac)
    struct = jax.ShapeDtypeStruct

    records = call(
        records_body, struct((peers, 1, SLOT * STRIDE), f32),
        (pltpu.VMEM((LANES, slots), f32), pltpu.VMEM((slots, LANES), f32), pltpu.VMEM((peers, SLOT * STRIDE), f32)),
    )(obs.reshape(CH, 1, slots), obs_weight.reshape(CH, 1, slots), fp_class)
    records = lax.all_to_all(records, "lat", split_axis=0, concat_axis=0, tiled=True)

    edge = struct((depth, LANES), f32)
    first, last, to_right, to_left = call(edges_body, (edge, edge, edge, edge))(inc)
    up = moved(last, "lat", 1, False)
    down = moved(first, "lat", -1, False)
    from_left = moved(to_right, "lon", 1, True)
    from_right = moved(to_left, "lon", -1, True)

    seen, meta = call(
        state_body, (struct((kinds, LANES), f32), struct((8, LANES), f32)),
    )(inc, up, down, from_left, from_right, fp_col.reshape(1, slots), mixing_mask, mix, jac)
    own = call(
        departures_body, struct((24, LANES), f32),
        (pltpu.VMEM((8, SLOT * STRIDE), f32), pltpu.VMEM((LANES, LANES), f32)),
    )(records, seen, meta)

    above = moved(own, "lat", 1, False)
    below = moved(own, "lat", -1, False)
    lefts = moved(own, "lon", 1, True)
    rights = moved(own, "lon", -1, True)
    out = call(
        gradient_body, struct((depth * ROWS, LANES), f32),
        (pltpu.VMEM((kinds, 2 * LANES), f32), pltpu.VMEM((LANES, LANES), f32)),
    )(own, lefts, rights, above, below, turned_jac, mix, inc)
    return out.reshape(increment.shape)


def solution(mesh):
    return jax.shard_map(
        on_device,
        mesh=mesh,
        in_specs=(
            P(None, None, "lat", "lon"),
            P(),
            P("lat", "lon"),
            P(),
            P("lon", "lat", None),
            P("lon", "lat", None),
            P("lon", "lat", None, None),
            P("lon", "lat", None, None),
        ),
        out_specs=P(None, None, "lat", "lon"),
        check_vma=False,
    )
```

time: 187 us -> 84.7 us (0.45)
  the two profiles are of different devices: /device:TPU:31 before, /device:TPU:96 now
where the time goes in v1:
time: 84.7 us; the launch traced here: 84.2 us
  starting transfers between devices  58.8 us (69%)
  Pallas kernels  14 us (17%)
  waiting for transfers between devices  7.55 us (9%)
  local copies, waits for them, and re-layouts  3.79 us (4%)
    ppermute x8, starting transfers between devices, moved(): return lax.ppermute(x, axis, pairs)  31.1 us
    all_to_all x1, starting transfers between devices, on_device(): lax.all_to_all(records, 'lat', split_axis=0, concat_axis=0, tiled=True)  27.7 us
    ppermute x8, waiting for transfers between devices, moved(): return lax.ppermute(x, axis, pairs)  7.54 us
    pallas_call x1, Pallas kernels, on_device(): call(state_body, (struct((kinds, LANES), f32), struct((8, LANES), f32)))  4.18 us
    pallas_call x1, Pallas kernels, on_device(): call(gradient_body, struct((depth * ROWS, LANES), f32), (pltpu.VMEM((kind...  3.79 us
    pallas_call x1, Pallas kernels, on_device(): call(edges_body, (edge, edge, edge, edge))(inc)  2.57 us
    unnamed x22, local copies, waits for them, and re-layouts  1.86 us
    pallas_call x1, Pallas kernels, on_device(): call(departures_body, struct((24, LANES), f32), (pltpu.VMEM((8, SLOT * ST...  1.82 us
  transfers between devices with their start and end apart: 9, of which 3 were waited for; matrix products, arithmetic and copies ran while one was open for 2% of the time, Pallas kernels for 8%

profile of v1, /device:TPU:96, one launch (start us, length us, event | category | flops | bytes accessed | tf_op | source)
XLA Modules:
  0.0 84.2 jit_solution(12401038386329810677)
XLA Ops:
  0.0 1.6 %shard_map.82 = f32[32,1,384]{2,1,0:T(1,128)} custom-call(f32[20,1,256]{2,1,0:T(1,128)} %bitcast.15, f32[20,1,256]{2,1,0:T(1,128)} %bitcast.16, s32[1,1,256]{2,1,0:T(1,128)} %class_ref.1), custom_call_target="tpu_custom_call" | custom-call | flops 1000000 | bytes 1000000 | tf_op jit(solution)/shard_map/pallas_call | solution.py:260
  1.6 27.7 %all-to-all-start = ((f32[32,1,384]{2,1,0:T(1,128)}), f32[32,1,384]{2,1,0:T(1,128)S(1)}, u32[]{:S(2)}, u32[]{:S(2)}) async-start(f32[32,1,384]{2,1,0:T(1,128)} %shard_map.82), calls=%async_computation | async-start | bytes 98304 | tf_op jit(solution)/shard_map/all_to_all | solution.py:264
  29.3 2.6 %shard_map.83 = (f32[274,128]{1,0:T(8,128)}, f32[274,128]{1,0:T(8,128)}, f32[274,128]{1,0:T(8,128)}, f32[274,128]{1,0:T(8,128)}) custom-call(f32[2192,128]{1,0:T(8,128)} %bitcast.9), custom_call_target="tpu_custom_call" | custom-call | flops 1000000 | bytes 1000000 | tf_op jit(solution)/shard_map/pallas_call | solution.py:267
  31.9 4.6 %collective-permute-start = (f32[274,128]{1,0:T(8,128)}, f32[274,128]{1,0:T(8,128)S(1)}, u32[]{:S(2)}, u32[]{:S(2)}) collective-permute-start(f32[274,128]{1,0:T(8,128)} %get-tuple-element.11), channel_id=1, source_target_pairs={{0,1},{1,2},{2,3},{3,4},{4,5},{5,6},{6,7},{7,8},{8,9},{9,10},{10,1... | collective-permute-start | bytes 420872 | tf_op jit(solution)/shard_map/ppermute | solution.py:245
  36.5 1.9 %collective-permute-start.1 = (f32[274,128]{1,0:T(8,128)}, f32[274,128]{1,0:T(8,128)S(1)}, u32[]{:S(2)}, u32[]{:S(2)}) collective-permute-start(f32[274,128]{1,0:T(8,128)} %get-tuple-element.12), channel_id=1, source_target_pairs={{1,0},{2,1},{3,2},{4,3},{5,4},{6,5},{7,6},{8,7},{9,8},{10,9},{11,1... | collective-permute-start | bytes 420872 | tf_op jit(solution)/shard_map/ppermute | solution.py:245
  38.4 1.9 %collective-permute-start.2 = (f32[274,128]{1,0:T(8,128)}, f32[274,128]{1,0:T(8,128)S(1)}, u32[]{:S(2)}, u32[]{:S(2)}) collective-permute-start(f32[274,128]{1,0:T(8,128)} %get-tuple-element.13), channel_id=1, source_target_pairs={{0,32},{32,64},{64,96},{96,128},{128,160},{160,192},{192,224},{224... | collective-permute-start | bytes 420872 | tf_op jit(solution)/shard_map/ppermute | solution.py:245
  40.3 7.0 %collective-permute-start.3 = (f32[274,128]{1,0:T(8,128)}, f32[274,128]{1,0:T(8,128)S(1)}, u32[]{:S(2)}, u32[]{:S(2)}) collective-permute-start(f32[274,128]{1,0:T(8,128)} %get-tuple-element.14), channel_id=1, source_target_pairs={{0,992},{32,0},{64,32},{96,64},{128,96},{160,128},{192,160},{224,1... | collective-permute-start | bytes 420872 | tf_op jit(solution)/shard_map/ppermute | solution.py:245
  47.3 0.9 %reshape.28.mix_ref = f32[274,1]{1,0:T(8,128)} reshape(f32[2,137]{1,0:T(2,128)S(1)} %copy-done.10) | data formatting | bytes 2192 | tf_op jit(solution)/shard_map/reshape | solution.py:255
  48.2 0.2 collective-permute-done.2.from_left_ref
  48.3 1.9 %collective-permute-done.3.from_right_ref = f32[274,128]{1,0:T(8,128)S(1)} collective-permute-done((f32[274,128]{1,0:T(8,128)}, f32[274,128]{1,0:T(8,128)S(1)}, u32[]{:S(2)}, u32[]{:S(2)}) %collective-permute-start.3) | collective-permute-done | bytes 140320 | tf_op jit(solution)/shard_map/ppermute | solution.py:245
  50.2 0.6 copy-done.5
  50.9 4.2 %shard_map.84 = (f32[800,128]{1,0:T(8,128)}, f32[8,128]{1,0:T(8,128)}) custom-call(f32[2192,128]{1,0:T(8,128)} %bitcast.10, f32[274,128]{1,0:T(8,128)} %copy-done.2, f32[274,128]{1,0:T(8,128)} %copy-done.3, f32[274,128]{1,0:T(8,128)} %copy-done.4, f32[274,128]{1,0:T(8,128)} %copy-done.5, s32[1,256]{1,0:T(1,128)} %bitcast.17, s32[8,128]{1,0:T(8,128)} %mask_ref.1, ...), custom_call_target="tpu_custom_call" | custom-call | flops 1000000 | bytes 1000000 | tf_op jit(solution)/shard_map/pallas_call | solution.py:273
  55.1 0.0 all-to-all-done.records_ref
  55.1 0.6 copy-done.1
  55.7 1.8 %shard_map.85.own_ref = f32[24,128]{1,0:T(8,128)} custom-call(f32[32,1,384]{2,1,0:T(1,128)} %copy-done.1, f32[800,128]{1,0:T(8,128)} %get-tuple-element.15.seen_ref, f32[8,128]{1,0:T(8,128)} %get-tuple-element.16.meta_ref), custom_call_target="tpu_custom_call" | custom-call | flops 1000000 | bytes 1000000 | tf_op jit(solution)/shard_map/pallas_call | solution.py:276
  57.5 1.9 %collective-permute-start.7 = (f32[24,128]{1,0:T(8,128)}, f32[24,128]{1,0:T(8,128)S(1)}, u32[]{:S(2)}, u32[]{:S(2)}) collective-permute-start(f32[24,128]{1,0:T(8,128)} %shard_map.85.own_ref), channel_id=1, source_target_pairs={{1,0},{2,1},{3,2},{4,3},{5,4},{6,5},{7,6},{8,7},{9,8},{10,9},{11,1... | collective-permute-start | bytes 36872 | tf_op jit(solution)/shard_map/ppermute | solution.py:245
  59.4 5.1 %collective-permute-start.6 = (f32[24,128]{1,0:T(8,128)}, f32[24,128]{1,0:T(8,128)S(1)}, u32[]{:S(2)}, u32[]{:S(2)}) collective-permute-start(f32[24,128]{1,0:T(8,128)} %shard_map.85.own_ref), channel_id=1, source_target_pairs={{0,1},{1,2},{2,3},{3,4},{4,5},{5,6},{6,7},{7,8},{8,9},{9,10},{10,1... | collective-permute-start | bytes 36872 | tf_op jit(solution)/shard_map/ppermute | solution.py:245
  64.5 6.7 %collective-permute-start.5 = (f32[24,128]{1,0:T(8,128)}, f32[24,128]{1,0:T(8,128)S(1)}, u32[]{:S(2)}, u32[]{:S(2)}) collective-permute-start(f32[24,128]{1,0:T(8,128)} %shard_map.85.own_ref), channel_id=1, source_target_pairs={{0,992},{32,0},{64,32},{96,64},{128,96},{160,128},{192,160},{224,1... | collective-permute-start | bytes 36872 | tf_op jit(solution)/shard_map/ppermute | solution.py:245
  71.3 1.9 %collective-permute-start.4 = (f32[24,128]{1,0:T(8,128)}, f32[24,128]{1,0:T(8,128)S(1)}, u32[]{:S(2)}, u32[]{:S(2)}) collective-permute-start(f32[24,128]{1,0:T(8,128)} %shard_map.85.own_ref), channel_id=1, source_target_pairs={{0,32},{32,64},{64,96},{96,128},{128,160},{160,192},{192,224},{224... | collective-permute-start | bytes 36872 | tf_op jit(solution)/shard_map/ppermute | solution.py:245
  73.2 1.1 %copy.12 = bf16[800,274]{0,1:T(8,128)(2,1)} copy(bf16[800,274]{1,0:T(8,128)(2,1)S(1)} %bitcast.13) | data formatting | bytes 876800 | tf_op jit(solution)/shard_map/reshape | solution.py:256
  74.3 0.0 collective-permute-done.6.up_ref
  74.3 5.5 %collective-permute-done.4.left_ref = f32[24,128]{1,0:T(8,128)S(1)} collective-permute-done((f32[24,128]{1,0:T(8,128)}, f32[24,128]{1,0:T(8,128)S(1)}, u32[]{:S(2)}, u32[]{:S(2)}) %collective-permute-start.4) | collective-permute-done | bytes 12320 | tf_op jit(solution)/shard_map/ppermute | solution.py:245
  79.9 0.6 copy-done.9
  80.4 3.8 %shard_map.86 = f32[2192,128]{1,0:T(8,128)} custom-call(f32[24,128]{1,0:T(8,128)} %shard_map.85.own_ref, f32[24,128]{1,0:T(8,128)} %copy-done.9, f32[24,128]{1,0:T(8,128)} %copy-done.8, f32[24,128]{1,0:T(8,128)} %copy-done.7, f32[24,128]{1,0:T(8,128)} %copy-done.6, bf16[274,800]{1,0:T(8,128)(2,1)} %bitcast.14, f32[274,1]{1,0:T(8,128)} %reshape.28.mix_ref, ...), custom_call_target="tpu_custom_call" | custom-call | flops 1000000 | bytes 1000000 | tf_op jit(solution)/shard_map/pallas_call | solution.py:285
  (23 shorter events, 0.0 us)
Async XLA Ops:
  0.0 47.3 %copy-start.10 = (f32[2,137]{1,0:T(2,128)S(1)}, f32[2,137]{1,0:T(2,128)}, u32[]{:S(2)}) copy-start(f32[2,137]{1,0:T(2,128)} %param.9) | copy-start | bytes 3292
  1.6 53.4 %all-to-all-start = ((f32[32,1,384]{2,1,0:T(1,128)}), f32[32,1,384]{2,1,0:T(1,128)S(1)}, u32[]{:S(2)}, u32[]{:S(2)}) async-start(f32[32,1,384]{2,1,0:T(1,128)} %shard_map.82), calls=%async_computation | async-start | bytes 98304 | tf_op jit(solution)/shard_map/all_to_all | solution.py:264
  31.9 16.3 %collective-permute-start = (f32[274,128]{1,0:T(8,128)}, f32[274,128]{1,0:T(8,128)S(1)}, u32[]{:S(2)}, u32[]{:S(2)}) collective-permute-start(f32[274,128]{1,0:T(8,128)} %get-tuple-element.11), channel_id=1, source_target_pairs={{0,1},{1,2},{2,3},{3,4},{4,5},{5,6},{6,7},{7,8},{8,9},{9,10},{10,1... | collective-permute-start | bytes 420872 | tf_op jit(solution)/shard_map/ppermute | solution.py:245
  36.5 11.7 %collective-permute-start.1 = (f32[274,128]{1,0:T(8,128)}, f32[274,128]{1,0:T(8,128)S(1)}, u32[]{:S(2)}, u32[]{:S(2)}) collective-permute-start(f32[274,128]{1,0:T(8,128)} %get-tuple-element.12), channel_id=1, source_target_pairs={{1,0},{2,1},{3,2},{4,3},{5,4},{6,5},{7,6},{8,7},{9,8},{10,9},{11,1... | collective-permute-start | bytes 420872 | tf_op jit(solution)/shard_map/ppermute | solution.py:245
  38.4 9.9 %collective-permute-start.2 = (f32[274,128]{1,0:T(8,128)}, f32[274,128]{1,0:T(8,128)S(1)}, u32[]{:S(2)}, u32[]{:S(2)}) collective-permute-start(f32[274,128]{1,0:T(8,128)} %get-tuple-element.13), channel_id=1, source_target_pairs={{0,32},{32,64},{64,96},{96,128},{128,160},{160,192},{192,224},{224... | collective-permute-start | bytes 420872 | tf_op jit(solution)/shard_map/ppermute | solution.py:245
  40.3 9.9 %collective-permute-start.3 = (f32[274,128]{1,0:T(8,128)}, f32[274,128]{1,0:T(8,128)S(1)}, u32[]{:S(2)}, u32[]{:S(2)}) collective-permute-start(f32[274,128]{1,0:T(8,128)} %get-tuple-element.14), channel_id=1, source_target_pairs={{0,992},{32,0},{64,32},{96,64},{128,96},{160,128},{192,160},{224,1... | collective-permute-start | bytes 420872 | tf_op jit(solution)/shard_map/ppermute | solution.py:245
  48.2 2.1 %copy-start.2 = (f32[274,128]{1,0:T(8,128)}, f32[274,128]{1,0:T(8,128)S(1)}, u32[]{:S(2)}) copy-start(f32[274,128]{1,0:T(8,128)S(1)} %collective-permute-done.up_ref) | copy-start | bytes 420868
  48.2 2.0 %copy-start.3 = (f32[274,128]{1,0:T(8,128)}, f32[274,128]{1,0:T(8,128)S(1)}, u32[]{:S(2)}) copy-start(f32[274,128]{1,0:T(8,128)S(1)} %collective-permute-done.1.down_ref) | copy-start | bytes 420868
  48.3 1.9 %copy-start.4 = (f32[274,128]{1,0:T(8,128)}, f32[274,128]{1,0:T(8,128)S(1)}, u32[]{:S(2)}) copy-start(f32[274,128]{1,0:T(8,128)S(1)} %collective-permute-done.2.from_left_ref) | copy-start | bytes 420868
  50.2 0.6 copy-start.5
  50.9 22.4 %copy-start = (bf16[40,20,274]{2,0,1:T(8,128)(2,1)S(1)}, bf16[40,20,274]{2,0,1:T(8,128)(2,1)}, u32[]{:S(2)}) copy-start(bf16[40,20,274]{2,0,1:T(8,128)(2,1)} %param.11) | copy-start | bytes 1315204
  55.1 0.6 copy-start.1
  57.5 16.8 %collective-permute-start.7 = (f32[24,128]{1,0:T(8,128)}, f32[24,128]{1,0:T(8,128)S(1)}, u32[]{:S(2)}, u32[]{:S(2)}) collective-permute-start(f32[24,128]{1,0:T(8,128)} %shard_map.85.own_ref), channel_id=1, source_target_pairs={{1,0},{2,1},{3,2},{4,3},{5,4},{6,5},{7,6},{8,7},{9,8},{10,9},{11,1... | collective-permute-start | bytes 36872 | tf_op jit(solution)/shard_map/ppermute | solution.py:245
  59.4 14.9 %collective-permute-start.6 = (f32[24,128]{1,0:T(8,128)}, f32[24,128]{1,0:T(8,128)S(1)}, u32[]{:S(2)}, u32[]{:S(2)}) collective-permute-start(f32[24,128]{1,0:T(8,128)} %shard_map.85.own_ref), channel_id=1, source_target_pairs={{0,1},{1,2},{2,3},{3,4},{4,5},{5,6},{6,7},{7,8},{8,9},{9,10},{10,1... | collective-permute-start | bytes 36872 | tf_op jit(solution)/shard_map/ppermute | solution.py:245
  64.5 9.8 %collective-permute-start.5 = (f32[24,128]{1,0:T(8,128)}, f32[24,128]{1,0:T(8,128)S(1)}, u32[]{:S(2)}, u32[]{:S(2)}) collective-permute-start(f32[24,128]{1,0:T(8,128)} %shard_map.85.own_ref), channel_id=1, source_target_pairs={{0,992},{32,0},{64,32},{96,64},{128,96},{160,128},{192,160},{224,1... | collective-permute-start | bytes 36872 | tf_op jit(solution)/shard_map/ppermute | solution.py:245
  71.3 8.5 %collective-permute-start.4 = (f32[24,128]{1,0:T(8,128)}, f32[24,128]{1,0:T(8,128)S(1)}, u32[]{:S(2)}, u32[]{:S(2)}) collective-permute-start(f32[24,128]{1,0:T(8,128)} %shard_map.85.own_ref), channel_id=1, source_target_pairs={{0,32},{32,64},{64,96},{96,128},{128,160},{160,192},{192,224},{224... | collective-permute-start | bytes 36872 | tf_op jit(solution)/shard_map/ppermute | solution.py:245
  74.3 5.5 %copy-start.6 = (f32[24,128]{1,0:T(8,128)}, f32[24,128]{1,0:T(8,128)S(1)}, u32[]{:S(2)}) copy-start(f32[24,128]{1,0:T(8,128)S(1)} %collective-permute-done.7.down_ref) | copy-start | bytes 36868
  74.3 5.5 %copy-start.7 = (f32[24,128]{1,0:T(8,128)}, f32[24,128]{1,0:T(8,128)S(1)}, u32[]{:S(2)}) copy-start(f32[24,128]{1,0:T(8,128)S(1)} %collective-permute-done.6.up_ref) | copy-start | bytes 36868
  74.3 5.5 %copy-start.8 = (f32[24,128]{1,0:T(8,128)}, f32[24,128]{1,0:T(8,128)S(1)}, u32[]{:S(2)}) copy-start(f32[24,128]{1,0:T(8,128)S(1)} %collective-permute-done.5.right_ref) | copy-start | bytes 36868
  79.8 0.6 copy-start.9

commit v2 on v1

--- a/solution.py
+++ b/solution.py
@@ -18,11 +18,15 @@
     return lax.broadcasted_iota(jnp.int32, shape, dim)
 
 
-def call(body, out_shape, scratch=(), flops=1000000):
+def call(body, out_shape, scratch=(), flops=1000000, inputs=1, limit=16 * 1024 * 1024):
+    vmem = pl.BlockSpec(memory_space=pltpu.VMEM)
     return pl.pallas_call(
         body,
         out_shape=out_shape,
+        in_specs=[vmem] * inputs,
+        out_specs=jax.tree.map(lambda _: vmem, out_shape),
         scratch_shapes=list(scratch),
+        compiler_params=pltpu.CompilerParams(vmem_limit_bytes=limit),
         cost_estimate=pl.CostEstimate(flops=flops, bytes_accessed=1000000, transcendentals=0),
     )
 
@@ -55,26 +59,34 @@
         out_ref[s] = flat_ref[s : s + 1, :]
 
 
-def edges_body(inc_ref, first_ref, last_ref, right_ref, left_ref):
-    depth = first_ref.shape[0]
+def is_even(axis):
+    return lax.axis_index(axis) % 2 == 0
+
+
+def edges_body(inc_ref, lon_ref, lat_ref, lat2_ref, lon2_ref):
+    depth = lon_ref.shape[0]
     lane = iota((depth, LANES), 1)
     right = jnp.zeros((depth, LANES), jnp.float32)
     left = jnp.zeros((depth, LANES), jnp.float32)
     for r in range(ROWS):
         row = inc_ref[pl.ds(r, depth, stride=ROWS), :]
         if r == 0:
-            first_ref[...] = row
+            first = row
         if r == ROWS - 1:
-            last_ref[...] = row
+            last = row
         right = jnp.where(lane == r, pltpu.roll(row, r + 1, 1), right)
         left = jnp.where(lane == ROWS + r, pltpu.roll(row, ROWS + r, 1), left)
-    right_ref[...] = right
-    left_ref[...] = left
-
-
-def state_body(inc_ref, up_ref, down_ref, from_left_ref, from_right_ref, col_ref, mask_ref,
-               mix_ref, jac_ref, seen_ref, meta_ref):
-    depth = up_ref.shape[0]
+    even = is_even("lat")
+    lat_ref[...] = jnp.where(even, last, first)
+    lat2_ref[...] = jnp.where(even, first, last)
+    even = is_even("lon")
+    lon_ref[...] = jnp.where(even, right, left)
+    lon2_ref[...] = jnp.where(even, left, right)
+
+
+def state_body(inc_ref, lon_ref, lat_ref, lat2_ref, lon2_ref, col_ref, mask_ref, mix_ref,
+               jac_ref, seen_ref, meta_ref):
+    depth = lat_ref.shape[0]
     lane8 = iota((8, LANES), 1)
     cols = jnp.full((8, LANES), NOWHERE, jnp.int32)
     owners = col_ref.shape[1] // (SLOT * OWN_EVERY)
@@ -111,14 +123,15 @@
         mask_row = jnp.broadcast_to(mask_ref[r : r + 1, :].astype(jnp.bfloat16), (8, LANES))
         masked = masked + jnp.dot(mask_row, chosen, preferred_element_type=jnp.float32)
     near = ~plain
-    chosen = jnp.where(near & (want == sub), 1.0, 0.0).astype(jnp.bfloat16)
-    total = total + split_dot(up_ref[...], chosen)
-    chosen = jnp.where(near & (want == sub + (ROWS - 1) * LANES), 1.0, 0.0).astype(jnp.bfloat16)
-    total = total + split_dot(down_ref[...], chosen)
+    meets = jnp.where(is_even("lat"), (ROWS - 1) * LANES, 0)
+    chosen = jnp.where(near & (want == sub + meets), 1.0, 0.0).astype(jnp.bfloat16)
+    total = total + split_dot(lat_ref[...], chosen)
+    chosen = jnp.where(near & (want == sub + ((ROWS - 1) * LANES - meets)), 1.0, 0.0).astype(jnp.bfloat16)
+    total = total + split_dot(lat2_ref[...], chosen)
     on_left = (sub < ROWS) & (want == sub * LANES)
     on_right = (sub >= ROWS) & (sub < 2 * ROWS) & (want == (sub - ROWS) * LANES + LANES - 1)
     chosen = jnp.where(near & (on_left | on_right), 1.0, 0.0).astype(jnp.bfloat16)
-    total = total + split_dot(from_left_ref[...] + from_right_ref[...], chosen)
+    total = total + split_dot(lon_ref[...] + lon2_ref[...], chosen)
 
     state = total + mix_ref[...] * masked[0:1, :] * pltpu.roll(total, LANES - 32, 1)
     state = jnp.where(iota((depth, LANES), 1) < 32, state, 0.0).astype(jnp.bfloat16)
@@ -159,15 +172,33 @@
     out_ref[CH : CH + 1, :] = jnp.where(live, kind, 0.0)
     out_ref[CH + 1 : CH + 2, :] = jnp.where(live, meta_ref[0:1, :], 0.0)
     out_ref[CH + 2 : CH + 3, :] = jnp.where(live, meta_ref[1:2, :], 0.0)
-
-
-def gradient_body(own_ref, left_ref, right_ref, up_ref, down_ref, turned_jac_ref, mix_ref, inc_ref,
+    col = meta_ref[0:1, :].astype(jnp.int32)
+    across = col & (LANES - 1)
+    ahead = [
+        jnp.where(across == LANES - 1, col - (LANES - 1), NOWHERE),
+        jnp.where(col >= (ROWS - 1) * LANES, col - (ROWS - 1) * LANES, NOWHERE),
+    ]
+    behind = [
+        jnp.where(across == 0, col + (LANES - 1), NOWHERE),
+        jnp.where((col >= 0) & (col < LANES), col + (ROWS - 1) * LANES, NOWHERE),
+    ]
+    for i, axis in enumerate(("lon", "lat")):
+        even = is_even(axis)
+        for j, swap in enumerate((even, jnp.logical_not(even))):
+            spot = jnp.where(swap, ahead[i], behind[i]).astype(jnp.float32)
+            row = CH + 3 + 2 * i + j
+            out_ref[row : row + 1, :] = jnp.where(live, spot, 0.0)
+
+
+def gradient_body(own_ref, lon2_ref, lat2_ref, lat_ref, lon_ref, turned_jac_ref, mix_ref, inc_ref,
                   out_ref, spread_ref, flip_ref):
     depth = turned_jac_ref.shape[0]
     classes = turned_jac_ref.shape[1] // CH
-    four = own_ref[...] + pltpu.roll(left_ref[...], 32, 1) + pltpu.roll(right_ref[...], 64, 1)
-    four = four + pltpu.roll(up_ref[...], 96, 1)
-    both = jnp.concatenate([four, down_ref[...]], 1)
+    lon = pltpu.roll(lon_ref[...], 32, 1)
+    lon2 = pltpu.roll(lon2_ref[...], 64, 1)
+    lat = pltpu.roll(lat_ref[...], 96, 1)
+    four = own_ref[...] + lon + lon2 + lat
+    both = jnp.concatenate([four, lat2_ref[...]], 1)
     kinds = jnp.broadcast_to(both[CH : CH + 1, :], (classes, 2 * LANES)).astype(jnp.int32)
     chosen = kinds == iota((classes, 2 * LANES), 0)
     for ch in range(CH):
@@ -191,45 +222,39 @@
     ).astype(jnp.bfloat16)
 
     flip_ref[...] = jnp.zeros(flip_ref.shape, jnp.float32)
-    lane1 = iota((1, LANES), 1)
-    own_col = own_ref[CH + 1 : CH + 2, :]
-    thrice = own_col + pltpu.roll(jnp.broadcast_to(own_col, (8, LANES)), 32, 1)[0:1, :]
-    thrice = thrice + pltpu.roll(jnp.broadcast_to(own_col, (8, LANES)), 64, 1)[0:1, :]
-    flip_ref[0:1, :] = jnp.where(lane1 < 96, thrice, float(NOWHERE))
-    flip_ref[1:2, :] = four[CH + 1 : CH + 2, :]
+    lane8 = iota((8, LANES), 1)
+    own_col = jnp.broadcast_to(own_ref[CH + 1 : CH + 2, :], (8, LANES))
+    thrice = own_col + pltpu.roll(own_col, 32, 1) + pltpu.roll(own_col, 64, 1)
+    flip_ref[0:8, :] = jnp.where(lane8 < 96, thrice, float(NOWHERE))
+    spots = own_ref[CH + 1 : CH + 2, :] + lon[CH + 3 : CH + 4, :] + lon2[CH + 4 : CH + 5, :] + lat[CH + 5 : CH + 6, :]
+    flip_ref[1:2, :] = spots
     flip_ref[2:3, :] = four[CH + 2 : CH + 3, :]
-    down_col = jnp.broadcast_to(down_ref[CH + 1 : CH + 2, :], (8, LANES))
-    down_on = jnp.broadcast_to(down_ref[CH + 2 : CH + 3, :], (8, LANES))
-    flip_ref[3:4, :] = (down_col + pltpu.roll(down_col, 32, 1))[0:1, :]
-    flip_ref[4:5, :] = (down_on + pltpu.roll(down_on, 32, 1))[0:1, :]
+    lat2_spot = jnp.broadcast_to(lat2_ref[CH + 6 : CH + 7, :], (8, LANES))
+    lat2_on = jnp.broadcast_to(lat2_ref[CH + 2 : CH + 3, :], (8, LANES))
+    flip_ref[3:4, :] = (lat2_spot + pltpu.roll(lat2_spot, 32, 1))[0:1, :]
+    flip_ref[4:5, :] = (lat2_on + pltpu.roll(lat2_on, 32, 1))[0:1, :]
     flipped = jnp.transpose(flip_ref[...])
     col3 = jnp.broadcast_to(flipped[:, 0:1], (LANES, LANES)).astype(jnp.int32)
     col = jnp.broadcast_to(flipped[:, 1:2], (LANES, LANES)).astype(jnp.int32)
     on = jnp.broadcast_to(flipped[:, 2:3], (LANES, LANES))
-    col_down = jnp.broadcast_to(flipped[:, 3:4], (LANES, LANES)).astype(jnp.int32)
-    on_down = jnp.broadcast_to(flipped[:, 4:5], (LANES, LANES))
+    col_last = jnp.broadcast_to(flipped[:, 3:4], (LANES, LANES)).astype(jnp.int32)
+    on_last = jnp.broadcast_to(flipped[:, 4:5], (LANES, LANES))
     across = iota((LANES, LANES), 1)
     spot = iota((32, LANES), 1)
-    none = jnp.zeros((32, LANES), jnp.float32)
+    mine = col[0:32, :]
 
     def right_side(r):
         point = across + r * LANES
         pick = jnp.where(col3 == point, 1.0, 0.0)
-        mine, lefts, rights, ups = (col[32 * i : 32 * (i + 1), :] for i in range(4))
         here = spot + r * LANES
         stencil = jnp.where(mine == here, -4.0, 0.0)
         stencil = stencil + jnp.where((mine == here - 1) & (spot != 0), 1.0, 0.0)
         stencil = stencil + jnp.where((mine == here + 1) & (spot != LANES - 1), 1.0, 0.0)
         stencil = stencil + jnp.where((mine == here - LANES) | (mine == here + LANES), 1.0, 0.0)
-        to_left = jnp.where((spot == 0) & (lefts == r * LANES + LANES - 1), 1.0, 0.0)
-        to_right = jnp.where((spot == LANES - 1) & (rights == r * LANES), 1.0, 0.0)
-        to_up = jnp.where(ups == spot + (ROWS - 1) * LANES, 1.0, 0.0) if r == 0 else none
-        reach = jnp.concatenate([stencil, to_left, to_right, to_up], 0) * on
-        if r == ROWS - 1:
-            to_down = jnp.where(col_down == across, 1.0, 0.0) * on_down
-        else:
-            to_down = jnp.zeros((LANES, LANES), jnp.float32)
-        return jnp.concatenate([pick, reach, reach, to_down], 0).astype(jnp.bfloat16)
+        given = jnp.where(col[32:LANES, :] == point[32:LANES, :], 1.0, 0.0)
+        reach = jnp.concatenate([stencil, given], 0) * on
+        reach_last = jnp.where(col_last == point, on_last, 0.0)
+        return jnp.concatenate([pick, reach, reach, reach_last], 0).astype(jnp.bfloat16)
 
     for r in range(0, ROWS, 2):
         pair = jnp.concatenate([right_side(r), right_side(r + 1)], 1)
@@ -239,9 +264,12 @@
             out_ref[rows, :] = inc_ref[rows, :] + added[:, i * LANES : (i + 1) * LANES]
 
 
-def moved(x, axis, step, periodic):
+def swapped(x, axis, start, periodic):
     count = lax.axis_size(axis)
-    pairs = [(i, (i + step) % count) for i in range(count) if periodic or 0 <= i + step < count]
+    pairs = []
+    for i in range(start, count, 2):
+        if periodic or i + 1 < count:
+            pairs += [(i, (i + 1) % count), ((i + 1) % count, i)]
     return lax.ppermute(x, axis, pairs)
 
 
@@ -260,32 +288,27 @@
     records = call(
         records_body, struct((peers, 1, SLOT * STRIDE), f32),
         (pltpu.VMEM((LANES, slots), f32), pltpu.VMEM((slots, LANES), f32), pltpu.VMEM((peers, SLOT * STRIDE), f32)),
+        inputs=3, limit=None,
     )(obs.reshape(CH, 1, slots), obs_weight.reshape(CH, 1, slots), fp_class)
     records = lax.all_to_all(records, "lat", split_axis=0, concat_axis=0, tiled=True)
 
     edge = struct((depth, LANES), f32)
-    first, last, to_right, to_left = call(edges_body, (edge, edge, edge, edge))(inc)
-    up = moved(last, "lat", 1, False)
-    down = moved(first, "lat", -1, False)
-    from_left = moved(to_right, "lon", 1, True)
-    from_right = moved(to_left, "lon", -1, True)
+    edges = call(edges_body, (edge, edge, edge, edge))(inc)
+    swaps = (("lon", 0, True), ("lat", 0, False), ("lat", 1, False), ("lon", 1, True))
+    edges = [swapped(x, *swap) for x, swap in zip(edges, swaps)]
 
     seen, meta = call(
-        state_body, (struct((kinds, LANES), f32), struct((8, LANES), f32)),
-    )(inc, up, down, from_left, from_right, fp_col.reshape(1, slots), mixing_mask, mix, jac)
+        state_body, (struct((kinds, LANES), f32), struct((8, LANES), f32)), inputs=9,
+    )(inc, *edges, fp_col.reshape(1, slots), mixing_mask, mix, jac)
     own = call(
-        departures_body, struct((24, LANES), f32),
-        (pltpu.VMEM((8, SLOT * STRIDE), f32), pltpu.VMEM((LANES, LANES), f32)),
+        departures_body, struct((32, LANES), f32),
+        (pltpu.VMEM((8, SLOT * STRIDE), f32), pltpu.VMEM((LANES, LANES), f32)), inputs=3,
     )(records, seen, meta)
 
-    above = moved(own, "lat", 1, False)
-    below = moved(own, "lat", -1, False)
-    lefts = moved(own, "lon", 1, True)
-    rights = moved(own, "lon", -1, True)
     out = call(
         gradient_body, struct((depth * ROWS, LANES), f32),
-        (pltpu.VMEM((kinds, 2 * LANES), f32), pltpu.VMEM((LANES, LANES), f32)),
-    )(own, lefts, rights, above, below, turned_jac, mix, inc)
+        (pltpu.VMEM((kinds, 2 * LANES), f32), pltpu.VMEM((LANES, LANES), f32)), inputs=8,
+    )(own, *(swapped(own, *swap) for swap in swaps[::-1]), turned_jac, mix, inc)
     return out.reshape(increment.shape)
 
 

time: 84.7 us -> 74.6 us (0.88)
  the two profiles are of different devices: /device:TPU:96 before, /device:TPU:32 now
where the time goes in v2:
time: 74.6 us; the launch traced here: 74.2 us
  starting transfers between devices  59.8 us (80%)
  Pallas kernels  6.46 us (9%)
  waiting for transfers between devices  4.9 us (7%)
  local copies, waits for them, and re-layouts  2.84 us (4%)
    ppermute x8, starting transfers between devices, swapped(): return lax.ppermute(x, axis, pairs)  31.2 us
    all_to_all x1, starting transfers between devices, on_device(): lax.all_to_all(records, 'lat', split_axis=0, concat_axis=0, tiled=True)  28.6 us
    ppermute x8, waiting for transfers between devices, swapped(): return lax.ppermute(x, axis, pairs)  4.67 us
    unnamed x14, local copies, waits for them, and re-layouts  2.33 us
    pallas_call x1, Pallas kernels, on_device(): call(gradient_body, struct((depth * ROWS, LANES), f32), (pltpu.VMEM((kind...  2.27 us
    pallas_call x1, Pallas kernels, on_device(): call(records_body, struct((peers, 1, SLOT * STRIDE), f32), (pltpu.VMEM((L...  1.64 us
    pallas_call x1, Pallas kernels, on_device(): call(state_body, (struct((kinds, LANES), f32), struct((8, LANES), f32)),...  1.63 us
  transfers between devices with their start and end apart: 9, of which 3 were waited for; matrix products, arithmetic and copies ran while one was open for 1% of the time, Pallas kernels for 3%

profile of v2, /device:TPU:32, one launch (start us, length us, event | category | flops | bytes accessed | tf_op | source)
XLA Modules:
  0.0 74.2 jit_solution(13846150509674373552)
XLA Ops:
  0.0 1.6 %shard_map.82 = f32[32,1,384]{2,1,0:T(1,128)} custom-call(f32[20,1,256]{2,1,0:T(1,128)} %bitcast.16, f32[20,1,256]{2,1,0:T(1,128)} %bitcast.17, s32[1,1,256]{2,1,0:T(1,128)} %class_ref.1), custom_call_target="tpu_custom_call" | custom-call | flops 1000000 | bytes 1000000 | tf_op jit(solution)/shard_map/pallas_call | solution.py:288
  1.6 28.6 %all-to-all-start = ((f32[32,1,384]{2,1,0:T(1,128)}), f32[32,1,384]{2,1,0:T(1,128)S(1)}, u32[]{:S(2)}, u32[]{:S(2)}) async-start(f32[32,1,384]{2,1,0:T(1,128)} %shard_map.82), calls=%async_computation | async-start | bytes 98304 | tf_op jit(solution)/shard_map/all_to_all | solution.py:293
  30.3 0.0 copy-start
  30.3 1.2 %copy-done = f32[2,137,8,128]{3,2,1,0:T(8,128)S(1)} copy-done((f32[2,137,8,128]{3,2,1,0:T(8,128)S(1)}, f32[2,137,8,128]{3,2,1,0:T(8,128)}, u32[]{:S(2)}) %copy-start) | copy-done | bytes 1122328
  31.5 0.7 shard_map.83
  32.2 1.9 %collective-permute-start = (f32[274,128]{1,0:T(8,128)S(1)}, f32[274,128]{1,0:T(8,128)S(1)}, u32[]{:S(2)}, u32[]{:S(2)}) collective-permute-start(f32[274,128]{1,0:T(8,128)S(1)} %get-tuple-element.11), channel_id=1, source_target_pairs={{0,32},{32,0},{64,96},{96,64},{128,160},{160,128},{192,224},{224,1... | collective-permute-start | bytes 420872 | tf_op jit(solution)/shard_map/ppermute | solution.py:273
  34.2 2.1 %collective-permute-start.1 = (f32[274,128]{1,0:T(8,128)S(1)}, f32[274,128]{1,0:T(8,128)S(1)}, u32[]{:S(2)}, u32[]{:S(2)}) collective-permute-start(f32[274,128]{1,0:T(8,128)S(1)} %get-tuple-element.12), channel_id=1, source_target_pairs={{0,1},{1,0},{2,3},{3,2},{4,5},{5,4},{6,7},{7,6},{8,9},{9,8},{10,11... | collective-permute-start | bytes 420872 | tf_op jit(solution)/shard_map/ppermute | solution.py:273
  36.3 4.6 %collective-permute-start.2 = (f32[274,128]{1,0:T(8,128)S(1)}, f32[274,128]{1,0:T(8,128)S(1)}, u32[]{:S(2)}, u32[]{:S(2)}) collective-permute-start(f32[274,128]{1,0:T(8,128)S(1)} %get-tuple-element.13), channel_id=1, source_target_pairs={{1,2},{2,1},{3,4},{4,3},{5,6},{6,5},{7,8},{8,7},{9,10},{10,9},{11,... | collective-permute-start | bytes 420872 | tf_op jit(solution)/shard_map/ppermute | solution.py:273
  40.9 6.7 %collective-permute-start.3 = (f32[274,128]{1,0:T(8,128)S(1)}, f32[274,128]{1,0:T(8,128)S(1)}, u32[]{:S(2)}, u32[]{:S(2)}) collective-permute-start(f32[274,128]{1,0:T(8,128)S(1)} %get-tuple-element.14), channel_id=1, source_target_pairs={{32,64},{64,32},{96,128},{128,96},{160,192},{192,160},{224,256},{2... | collective-permute-start | bytes 420872 | tf_op jit(solution)/shard_map/ppermute | solution.py:273
  47.6 0.2 reshape.28.mix_ref
  47.8 0.0 collective-permute-done.lon_ref
  47.8 2.8 %collective-permute-done.3.lon2_ref = f32[274,128]{1,0:T(8,128)S(1)} collective-permute-done((f32[274,128]{1,0:T(8,128)S(1)}, f32[274,128]{1,0:T(8,128)S(1)}, u32[]{:S(2)}, u32[]{:S(2)}) %collective-permute-start.3) | collective-permute-done | bytes 140320 | tf_op jit(solution)/shard_map/ppermute | solution.py:273
  50.7 0.0 copy-start.2
  50.7 1.1 %copy-done.2 = bf16[40,20,274]{2,0,1:T(8,128)(2,1)S(1)} copy-done((bf16[40,20,274]{2,0,1:T(8,128)(2,1)S(1)}, bf16[40,20,274]{2,0,1:T(8,128)(2,1)}, u32[]{:S(2)}) %copy-start.2) | copy-done | bytes 438424
  51.7 1.6 %shard_map.84 = (f32[800,128]{1,0:T(8,128)S(1)}, f32[8,128]{1,0:T(8,128)S(1)}) custom-call(f32[2192,128]{1,0:T(8,128)S(1)} %bitcast.10, f32[274,128]{1,0:T(8,128)S(1)} %collective-permute-done.lon_ref, f32[274,128]{1,0:T(8,128)S(1)} %collective-permute-done.1.lat_ref, f32[274,128]{1,0:T(8,128)S(1)} %collective-permute-done.2.lat2_ref, ...), custom_call_target="tpu_custom_call" | custom-call | flops 1000000 | bytes 1000000 | tf_op jit(solution)/shard_map/pallas_call | solution.py:300
  53.4 0.2 all-to-all-done.records_ref
  53.6 0.2 shard_map.85.own_ref
  53.8 1.9 %collective-permute-start.7 = (f32[32,128]{1,0:T(8,128)S(1)}, f32[32,128]{1,0:T(8,128)S(1)}, u32[]{:S(2)}, u32[]{:S(2)}) collective-permute-start(f32[32,128]{1,0:T(8,128)S(1)} %shard_map.85.own_ref), channel_id=1, source_target_pairs={{0,32},{32,0},{64,96},{96,64},{128,160},{160,128},{192,224},{224,1... | collective-permute-start | bytes 49160 | tf_op jit(solution)/shard_map/ppermute | solution.py:273
  55.7 3.3 %collective-permute-start.6 = (f32[32,128]{1,0:T(8,128)S(1)}, f32[32,128]{1,0:T(8,128)S(1)}, u32[]{:S(2)}, u32[]{:S(2)}) collective-permute-start(f32[32,128]{1,0:T(8,128)S(1)} %shard_map.85.own_ref), channel_id=1, source_target_pairs={{0,1},{1,0},{2,3},{3,2},{4,5},{5,4},{6,7},{7,6},{8,9},{9,8},{10,11... | collective-permute-start | bytes 49160 | tf_op jit(solution)/shard_map/ppermute | solution.py:273
  59.1 4.4 %collective-permute-start.5 = (f32[32,128]{1,0:T(8,128)S(1)}, f32[32,128]{1,0:T(8,128)S(1)}, u32[]{:S(2)}, u32[]{:S(2)}) collective-permute-start(f32[32,128]{1,0:T(8,128)S(1)} %shard_map.85.own_ref), channel_id=1, source_target_pairs={{1,2},{2,1},{3,4},{4,3},{5,6},{6,5},{7,8},{8,7},{9,10},{10,9},{11,... | collective-permute-start | bytes 49160 | tf_op jit(solution)/shard_map/ppermute | solution.py:273
  63.5 6.2 %collective-permute-start.4 = (f32[32,128]{1,0:T(8,128)S(1)}, f32[32,128]{1,0:T(8,128)S(1)}, u32[]{:S(2)}, u32[]{:S(2)}) collective-permute-start(f32[32,128]{1,0:T(8,128)S(1)} %shard_map.85.own_ref), channel_id=1, source_target_pairs={{32,64},{64,32},{96,128},{128,96},{160,192},{192,160},{224,256},{2... | collective-permute-start | bytes 49160 | tf_op jit(solution)/shard_map/ppermute | solution.py:273
  69.7 0.3 copy.12
  70.1 1.8 %collective-permute-done.4.lon2_ref = f32[32,128]{1,0:T(8,128)S(1)} collective-permute-done((f32[32,128]{1,0:T(8,128)S(1)}, f32[32,128]{1,0:T(8,128)S(1)}, u32[]{:S(2)}, u32[]{:S(2)}) %collective-permute-start.4) | collective-permute-done | bytes 16416 | tf_op jit(solution)/shard_map/ppermute | solution.py:273
  71.9 2.3 %shard_map.86 = f32[2192,128]{1,0:T(8,128)} custom-call(f32[32,128]{1,0:T(8,128)S(1)} %shard_map.85.own_ref, f32[32,128]{1,0:T(8,128)S(1)} %collective-permute-done.4.lon2_ref, f32[32,128]{1,0:T(8,128)S(1)} %collective-permute-done.5.lat2_ref, f32[32,128]{1,0:T(8,128)S(1)} %collective-permute-done.6.lat_ref, f32[32,128]{1,0:T(8,128)S(1)} %collective-permute-done.7.lon_ref, ...), custom_call_target="tpu_custom_call" | custom-call | flops 1000000 | bytes 1000000 | tf_op jit(solution)/shard_map/pallas_call | solution.py:308
  (15 shorter events, 0.0 us)
Async XLA Ops:
  0.0 47.6 %copy-start.6 = (f32[2,137]{1,0:T(2,128)S(1)}, f32[2,137]{1,0:T(2,128)}, u32[]{:S(2)}) copy-start(f32[2,137]{1,0:T(2,128)} %param.9) | copy-start | bytes 3292
  0.0 50.7 %copy-start.5 = (s32[1,1,256]{2,1,0:T(1,128)S(1)}, s32[1,1,256]{2,1,0:T(1,128)}, u32[]{:S(2)}) copy-start(s32[1,1,256]{2,1,0:T(1,128)} %param.12) | copy-start | bytes 3076
  0.0 50.7 %copy-start.4 = (s32[8,128]{1,0:T(8,128)S(1)}, s32[8,128]{1,0:T(8,128)}, u32[]{:S(2)}) copy-start(s32[8,128]{1,0:T(8,128)} %mask_ref.1) | copy-start | bytes 12292
  1.6 51.9 %all-to-all-start = ((f32[32,1,384]{2,1,0:T(1,128)}), f32[32,1,384]{2,1,0:T(1,128)S(1)}, u32[]{:S(2)}, u32[]{:S(2)}) async-start(f32[32,1,384]{2,1,0:T(1,128)} %shard_map.82), calls=%async_computation | async-start | bytes 98304 | tf_op jit(solution)/shard_map/all_to_all | solution.py:293
  30.3 1.3 %copy-start = (f32[2,137,8,128]{3,2,1,0:T(8,128)S(1)}, f32[2,137,8,128]{3,2,1,0:T(8,128)}, u32[]{:S(2)}) copy-start(f32[2,137,8,128]{3,2,1,0:T(8,128)} %param.8) | copy-start | bytes 3366916
  31.5 19.1 %copy-start.1 = (f32[2,137,8,128]{3,2,1,0:T(8,128)S(1)}, f32[2,137,8,128]{3,2,1,0:T(8,128)}, u32[]{:S(2)}) copy-start(f32[2,137,8,128]{3,2,1,0:T(8,128)} %param.8) | copy-start | bytes 3366916
  32.2 15.6 %collective-permute-start = (f32[274,128]{1,0:T(8,128)S(1)}, f32[274,128]{1,0:T(8,128)S(1)}, u32[]{:S(2)}, u32[]{:S(2)}) collective-permute-start(f32[274,128]{1,0:T(8,128)S(1)} %get-tuple-element.11), channel_id=1, source_target_pairs={{0,32},{32,0},{64,96},{96,64},{128,160},{160,128},{192,224},{224,1... | collective-permute-start | bytes 420872 | tf_op jit(solution)/shard_map/ppermute | solution.py:273
  34.2 13.7 %collective-permute-start.1 = (f32[274,128]{1,0:T(8,128)S(1)}, f32[274,128]{1,0:T(8,128)S(1)}, u32[]{:S(2)}, u32[]{:S(2)}) collective-permute-start(f32[274,128]{1,0:T(8,128)S(1)} %get-tuple-element.12), channel_id=1, source_target_pairs={{0,1},{1,0},{2,3},{3,2},{4,5},{5,4},{6,7},{7,6},{8,9},{9,8},{10,11... | collective-permute-start | bytes 420872 | tf_op jit(solution)/shard_map/ppermute | solution.py:273
  36.3 11.5 %collective-permute-start.2 = (f32[274,128]{1,0:T(8,128)S(1)}, f32[274,128]{1,0:T(8,128)S(1)}, u32[]{:S(2)}, u32[]{:S(2)}) collective-permute-start(f32[274,128]{1,0:T(8,128)S(1)} %get-tuple-element.13), channel_id=1, source_target_pairs={{1,2},{2,1},{3,4},{4,3},{5,6},{6,5},{7,8},{8,7},{9,10},{10,9},{11,... | collective-permute-start | bytes 420872 | tf_op jit(solution)/shard_map/ppermute | solution.py:273
  40.9 9.7 %collective-permute-start.3 = (f32[274,128]{1,0:T(8,128)S(1)}, f32[274,128]{1,0:T(8,128)S(1)}, u32[]{:S(2)}, u32[]{:S(2)}) collective-permute-start(f32[274,128]{1,0:T(8,128)S(1)} %get-tuple-element.14), channel_id=1, source_target_pairs={{32,64},{64,32},{96,128},{128,96},{160,192},{192,160},{224,256},{2... | collective-permute-start | bytes 420872 | tf_op jit(solution)/shard_map/ppermute | solution.py:273
  50.7 1.1 %copy-start.2 = (bf16[40,20,274]{2,0,1:T(8,128)(2,1)S(1)}, bf16[40,20,274]{2,0,1:T(8,128)(2,1)}, u32[]{:S(2)}) copy-start(bf16[40,20,274]{2,0,1:T(8,128)(2,1)} %param.11) | copy-start | bytes 1315204
  51.7 18.0 %copy-start.3 = (bf16[40,20,274]{2,0,1:T(8,128)(2,1)S(1)}, bf16[40,20,274]{2,0,1:T(8,128)(2,1)}, u32[]{:S(2)}) copy-start(bf16[40,20,274]{2,0,1:T(8,128)(2,1)} %param.11) | copy-start | bytes 1315204
  53.8 16.2 %collective-permute-start.7 = (f32[32,128]{1,0:T(8,128)S(1)}, f32[32,128]{1,0:T(8,128)S(1)}, u32[]{:S(2)}, u32[]{:S(2)}) collective-permute-start(f32[32,128]{1,0:T(8,128)S(1)} %shard_map.85.own_ref), channel_id=1, source_target_pairs={{0,32},{32,0},{64,96},{96,64},{128,160},{160,128},{192,224},{224,1... | collective-permute-start | bytes 49160 | tf_op jit(solution)/shard_map/ppermute | solution.py:273
  55.7 14.3 %collective-permute-start.6 = (f32[32,128]{1,0:T(8,128)S(1)}, f32[32,128]{1,0:T(8,128)S(1)}, u32[]{:S(2)}, u32[]{:S(2)}) collective-permute-start(f32[32,128]{1,0:T(8,128)S(1)} %shard_map.85.own_ref), channel_id=1, source_target_pairs={{0,1},{1,0},{2,3},{3,2},{4,5},{5,4},{6,7},{7,6},{8,9},{9,8},{10,11... | collective-permute-start | bytes 49160 | tf_op jit(solution)/shard_map/ppermute | solution.py:273
  59.1 11.0 %collective-permute-start.5 = (f32[32,128]{1,0:T(8,128)S(1)}, f32[32,128]{1,0:T(8,128)S(1)}, u32[]{:S(2)}, u32[]{:S(2)}) collective-permute-start(f32[32,128]{1,0:T(8,128)S(1)} %shard_map.85.own_ref), channel_id=1, source_target_pairs={{1,2},{2,1},{3,4},{4,3},{5,6},{6,5},{7,8},{8,7},{9,10},{10,9},{11,... | collective-permute-start | bytes 49160 | tf_op jit(solution)/shard_map/ppermute | solution.py:273
  63.5 8.4 %collective-permute-start.4 = (f32[32,128]{1,0:T(8,128)S(1)}, f32[32,128]{1,0:T(8,128)S(1)}, u32[]{:S(2)}, u32[]{:S(2)}) collective-permute-start(f32[32,128]{1,0:T(8,128)S(1)} %shard_map.85.own_ref), channel_id=1, source_target_pairs={{32,64},{64,32},{96,128},{128,96},{160,192},{192,160},{224,256},{2... | collective-permute-start | bytes 49160 | tf_op jit(solution)/shard_map/ppermute | solution.py:273

commit v3 on v2

--- a/solution.py
+++ b/solution.py
@@ -12,19 +12,20 @@
 STRIDE = 48
 CH = 20
 NOWHERE = -1000000
+CHUNK = 96
 
 
 def iota(shape, dim):
     return lax.broadcasted_iota(jnp.int32, shape, dim)
 
 
-def call(body, out_shape, scratch=(), flops=1000000, inputs=1, limit=16 * 1024 * 1024):
+def call(body, out_shape, scratch=(), flops=1000000, inputs=1, limit=16 * 1024 * 1024, space=pltpu.VMEM):
     vmem = pl.BlockSpec(memory_space=pltpu.VMEM)
     return pl.pallas_call(
         body,
         out_shape=out_shape,
         in_specs=[vmem] * inputs,
-        out_specs=jax.tree.map(lambda _: vmem, out_shape),
+        out_specs=jax.tree.map(lambda _: pl.BlockSpec(memory_space=space), out_shape),
         scratch_shapes=list(scratch),
         compiler_params=pltpu.CompilerParams(vmem_limit_bytes=limit),
         cost_estimate=pl.CostEstimate(flops=flops, bytes_accessed=1000000, transcendentals=0),
@@ -63,7 +64,7 @@
     return lax.axis_index(axis) % 2 == 0
 
 
-def edges_body(inc_ref, lon_ref, lat_ref, lat2_ref, lon2_ref):
+def edges_body(inc_ref, lon2_ref, lat_ref, lat2_ref, lon_ref):
     depth = lon_ref.shape[0]
     lane = iota((depth, LANES), 1)
     right = jnp.zeros((depth, LANES), jnp.float32)
@@ -84,7 +85,7 @@
     lon2_ref[...] = jnp.where(even, left, right)
 
 
-def state_body(inc_ref, lon_ref, lat_ref, lat2_ref, lon2_ref, col_ref, mask_ref, mix_ref,
+def state_body(inc_ref, lon2_ref, lat_ref, lat2_ref, lon_ref, col_ref, mask_ref, mix_ref,
                jac_ref, seen_ref, meta_ref):
     depth = lat_ref.shape[0]
     lane8 = iota((8, LANES), 1)
@@ -190,78 +191,67 @@
             out_ref[row : row + 1, :] = jnp.where(live, spot, 0.0)
 
 
-def gradient_body(own_ref, lon2_ref, lat2_ref, lat_ref, lon_ref, turned_jac_ref, mix_ref, inc_ref,
-                  out_ref, spread_ref, flip_ref):
+def gradient_body(own_ref, lon_ref, lat2_ref, lat_ref, lon2_ref, turned_jac_ref, mix_ref, inc_ref,
+                  out_hbm, spread_ref, flip_ref, out_ref, sems):
     depth = turned_jac_ref.shape[0]
     classes = turned_jac_ref.shape[1] // CH
-    lon = pltpu.roll(lon_ref[...], 32, 1)
-    lon2 = pltpu.roll(lon2_ref[...], 64, 1)
-    lat = pltpu.roll(lat_ref[...], 96, 1)
-    four = own_ref[...] + lon + lon2 + lat
-    both = jnp.concatenate([four, lat2_ref[...]], 1)
+    met = [ref[...] if i == 0 else pltpu.roll(ref[...], 32 * i, 1)
+           for i, ref in enumerate((lon_ref, lon2_ref, lat_ref, lat2_ref))]
+    others = met[0] + met[1] + met[2] + met[3]
+    both = jnp.concatenate([own_ref[...], others], 1)
     kinds = jnp.broadcast_to(both[CH : CH + 1, :], (classes, 2 * LANES)).astype(jnp.int32)
     chosen = kinds == iota((classes, 2 * LANES), 0)
     for ch in range(CH):
         spread_ref[ch * classes : (ch + 1) * classes, :] = jnp.where(chosen, both[ch : ch + 1, :], 0.0)
     adjoint = jnp.dot(turned_jac_ref[...], spread_ref[...].astype(jnp.bfloat16), preferred_element_type=jnp.float32)
 
-    lane = iota((depth, LANES), 1)
-    own = jnp.where(lane < 32, adjoint[:, 0:LANES], 0.0)
+    own = jnp.where(iota((depth, LANES), 1) < 32, adjoint[:, 0:LANES], 0.0)
     own_high = own.astype(jnp.bfloat16).astype(jnp.float32)
-    rest = own - own_high
-    own_mid = rest.astype(jnp.bfloat16).astype(jnp.float32)
-    own_low = rest - own_mid
-    summed = own_high + pltpu.roll(own_mid, 32, 1) + pltpu.roll(own_low, 64, 1)
-    mixed = mix_ref[...] * adjoint
+    mixed = mix_ref[...] * own
     mixed_high = mixed.astype(jnp.bfloat16).astype(jnp.float32)
-    mixed_low = mixed - mixed_high
-    last = jnp.where(lane < 32, mixed_high[:, LANES:], 0.0)
-    last = last + pltpu.roll(jnp.where(lane < 32, mixed_low[:, LANES:], 0.0), 32, 1)
-    left_side = jnp.concatenate(
-        [summed, mixed_high[:, 0:LANES], mixed_low[:, 0:LANES], last], 1
-    ).astype(jnp.bfloat16)
+    parts = own_high + pltpu.roll(own - own_high, 32, 1)
+    parts = parts + pltpu.roll(mixed_high, 64, 1) + pltpu.roll(mixed - mixed_high, 96, 1)
+    left_side = jnp.concatenate([parts, mix_ref[...] * adjoint[:, LANES:]], 1).astype(jnp.bfloat16)
 
     flip_ref[...] = jnp.zeros(flip_ref.shape, jnp.float32)
-    lane8 = iota((8, LANES), 1)
-    own_col = jnp.broadcast_to(own_ref[CH + 1 : CH + 2, :], (8, LANES))
-    thrice = own_col + pltpu.roll(own_col, 32, 1) + pltpu.roll(own_col, 64, 1)
-    flip_ref[0:8, :] = jnp.where(lane8 < 96, thrice, float(NOWHERE))
-    spots = own_ref[CH + 1 : CH + 2, :] + lon[CH + 3 : CH + 4, :] + lon2[CH + 4 : CH + 5, :] + lat[CH + 5 : CH + 6, :]
-    flip_ref[1:2, :] = spots
-    flip_ref[2:3, :] = four[CH + 2 : CH + 3, :]
-    lat2_spot = jnp.broadcast_to(lat2_ref[CH + 6 : CH + 7, :], (8, LANES))
-    lat2_on = jnp.broadcast_to(lat2_ref[CH + 2 : CH + 3, :], (8, LANES))
-    flip_ref[3:4, :] = (lat2_spot + pltpu.roll(lat2_spot, 32, 1))[0:1, :]
-    flip_ref[4:5, :] = (lat2_on + pltpu.roll(lat2_on, 32, 1))[0:1, :]
+    flip_ref[0:1, :] = own_ref[CH + 1 : CH + 2, :]
+    flip_ref[1:2, :] = own_ref[CH + 2 : CH + 3, :]
+    flip_ref[2:3, :] = sum(met[i][CH + 3 + n : CH + 4 + n, :] for i, n in enumerate((0, 1, 2, 3)))
+    flip_ref[3:4, :] = others[CH + 2 : CH + 3, :]
     flipped = jnp.transpose(flip_ref[...])
-    col3 = jnp.broadcast_to(flipped[:, 0:1], (LANES, LANES)).astype(jnp.int32)
-    col = jnp.broadcast_to(flipped[:, 1:2], (LANES, LANES)).astype(jnp.int32)
-    on = jnp.broadcast_to(flipped[:, 2:3], (LANES, LANES))
-    col_last = jnp.broadcast_to(flipped[:, 3:4], (LANES, LANES)).astype(jnp.int32)
-    on_last = jnp.broadcast_to(flipped[:, 4:5], (LANES, LANES))
+    mine = jnp.broadcast_to(flipped[0:32, 0:1], (32, LANES)).astype(jnp.int32)
+    on = jnp.broadcast_to(flipped[0:32, 1:2], (32, LANES))
+    theirs = jnp.broadcast_to(flipped[:, 2:3], (LANES, LANES)).astype(jnp.int32)
+    on_theirs = jnp.broadcast_to(flipped[:, 3:4], (LANES, LANES))
     across = iota((LANES, LANES), 1)
     spot = iota((32, LANES), 1)
-    mine = col[0:32, :]
 
     def right_side(r):
-        point = across + r * LANES
-        pick = jnp.where(col3 == point, 1.0, 0.0)
         here = spot + r * LANES
-        stencil = jnp.where(mine == here, -4.0, 0.0)
+        pick = jnp.where(mine == here, 1.0, 0.0)
+        stencil = -4.0 * pick
         stencil = stencil + jnp.where((mine == here - 1) & (spot != 0), 1.0, 0.0)
         stencil = stencil + jnp.where((mine == here + 1) & (spot != LANES - 1), 1.0, 0.0)
         stencil = stencil + jnp.where((mine == here - LANES) | (mine == here + LANES), 1.0, 0.0)
-        given = jnp.where(col[32:LANES, :] == point[32:LANES, :], 1.0, 0.0)
-        reach = jnp.concatenate([stencil, given], 0) * on
-        reach_last = jnp.where(col_last == point, on_last, 0.0)
-        return jnp.concatenate([pick, reach, reach, reach_last], 0).astype(jnp.bfloat16)
-
-    for r in range(0, ROWS, 2):
-        pair = jnp.concatenate([right_side(r), right_side(r + 1)], 1)
-        added = jnp.dot(left_side, pair, preferred_element_type=jnp.float32)
-        for i in range(2):
-            rows = pl.ds(r + i, depth, stride=ROWS)
-            out_ref[rows, :] = inc_ref[rows, :] + added[:, i * LANES : (i + 1) * LANES]
+        stencil = stencil * on
+        given = jnp.where(theirs == across + r * LANES, on_theirs, 0.0)
+        return jnp.concatenate([pick, pick, stencil, stencil, given], 0).astype(jnp.bfloat16)
+
+    right = [jnp.concatenate([right_side(r), right_side(r + 1)], 1) for r in range(0, ROWS, 2)]
+    copies = []
+    for n, first in enumerate(range(0, depth, CHUNK)):
+        size = min(CHUNK, depth - first)
+        part = left_side[first : first + size, :]
+        for r in range(0, ROWS, 2):
+            added = jnp.dot(part, right[r // 2], preferred_element_type=jnp.float32)
+            for i in range(2):
+                rows = pl.ds(first * ROWS + r + i, size, stride=ROWS)
+                out_ref[rows, :] = inc_ref[rows, :] + added[:, i * LANES : (i + 1) * LANES]
+        block = pl.ds(first * ROWS, size * ROWS)
+        copies.append(pltpu.make_async_copy(out_ref.at[block], out_hbm.at[block], sems.at[n]))
+        copies[-1].start()
+    for copy in copies:
+        copy.wait()
 
 
 def swapped(x, axis, start, periodic):
@@ -294,7 +284,7 @@
 
     edge = struct((depth, LANES), f32)
     edges = call(edges_body, (edge, edge, edge, edge))(inc)
-    swaps = (("lon", 0, True), ("lat", 0, False), ("lat", 1, False), ("lon", 1, True))
+    swaps = (("lon", 1, True), ("lat", 0, False), ("lat", 1, False), ("lon", 0, True))
     edges = [swapped(x, *swap) for x, swap in zip(edges, swaps)]
 
     seen, meta = call(
@@ -307,7 +297,9 @@
 
     out = call(
         gradient_body, struct((depth * ROWS, LANES), f32),
-        (pltpu.VMEM((kinds, 2 * LANES), f32), pltpu.VMEM((LANES, LANES), f32)), inputs=8,
+        (pltpu.VMEM((kinds, 2 * LANES), f32), pltpu.VMEM((LANES, LANES), f32),
+         pltpu.VMEM((depth * ROWS, LANES), f32), pltpu.SemaphoreType.DMA((pl.cdiv(depth, CHUNK),))),
+        inputs=8, space=pltpu.HBM,
     )(own, *(swapped(own, *swap) for swap in swaps[::-1]), turned_jac, mix, inc)
     return out.reshape(increment.shape)
 

time: 74.6 us -> 69.6 us (0.933)
  starting transfers between devices: 59.8 us -> 55.2 us
    ppermute x8, starting transfers between devices: 31.2 us -> 26.6 us  [swapped(): return lax.ppermute(x, axis, pairs)]
    ppermute x8, waiting for transfers between devices: 4.67 us -> 2.28 us  [swapped(): return lax.ppermute(x, axis, pairs)]
    all_to_all x1, waiting for transfers between devices: 0.22 us -> 2.62 us  [on_device(): lax.all_to_all(records, 'lat', split_axis=0, concat_axis=0, tiled=True)]
where the time goes in v3:
time: 69.6 us; the launch traced here: 69.1 us
  starting transfers between devices  55.2 us (79%)
  Pallas kernels  6.06 us (9%)
  waiting for transfers between devices  4.89 us (7%)
  local copies, waits for them, and re-layouts  2.84 us (4%)
    all_to_all x1, starting transfers between devices, on_device(): lax.all_to_all(records, 'lat', split_axis=0, concat_axis=0, tiled=True)  28.6 us
    ppermute x8, starting transfers between devices, swapped(): return lax.ppermute(x, axis, pairs)  26.6 us
    all_to_all x1, waiting for transfers between devices, on_device(): lax.all_to_all(records, 'lat', split_axis=0, concat_axis=0, tiled=True)  2.62 us
    unnamed x14, local copies, waits for them, and re-layouts  2.33 us
    ppermute x8, waiting for transfers between devices, swapped(): return lax.ppermute(x, axis, pairs)  2.28 us
    pallas_call x1, Pallas kernels, on_device(): call(gradient_body, struct((depth * ROWS, LANES), f32), (pltpu.VMEM((kind...  1.87 us
    pallas_call x1, Pallas kernels, on_device(): call(records_body, struct((peers, 1, SLOT * STRIDE), f32), (pltpu.VMEM((L...  1.64 us
    pallas_call x1, Pallas kernels, on_device(): call(state_body, (struct((kinds, LANES), f32), struct((8, LANES), f32)),...  1.63 us
  transfers between devices with their start and end apart: 9, of which 3 were waited for; matrix products, arithmetic and copies ran while one was open for 1% of the time, Pallas kernels for 3%

profile of v3, /device:TPU:32, one launch (start us, length us, event | category | flops | bytes accessed | tf_op | source)
XLA Modules:
  0.0 69.1 jit_solution(10634825413618484821)
XLA Ops:
  0.0 1.6 %shard_map.82 = f32[32,1,384]{2,1,0:T(1,128)} custom-call(f32[20,1,256]{2,1,0:T(1,128)} %bitcast.16, f32[20,1,256]{2,1,0:T(1,128)} %bitcast.17, s32[1,1,256]{2,1,0:T(1,128)} %class_ref.1), custom_call_target="tpu_custom_call" | custom-call | flops 1000000 | bytes 1000000 | tf_op jit(solution)/shard_map/pallas_call | solution.py:278
  1.6 28.6 %all-to-all-start = ((f32[32,1,384]{2,1,0:T(1,128)}), f32[32,1,384]{2,1,0:T(1,128)S(1)}, u32[]{:S(2)}, u32[]{:S(2)}) async-start(f32[32,1,384]{2,1,0:T(1,128)} %shard_map.82), calls=%async_computation | async-start | bytes 98304 | tf_op jit(solution)/shard_map/all_to_all | solution.py:283
  30.3 0.0 copy-start
  30.3 1.2 %copy-done = f32[2,137,8,128]{3,2,1,0:T(8,128)S(1)} copy-done((f32[2,137,8,128]{3,2,1,0:T(8,128)S(1)}, f32[2,137,8,128]{3,2,1,0:T(8,128)}, u32[]{:S(2)}) %copy-start) | copy-done | bytes 1122328
  31.5 0.7 %shard_map.83 = (f32[274,128]{1,0:T(8,128)S(1)}, f32[274,128]{1,0:T(8,128)S(1)}, f32[274,128]{1,0:T(8,128)S(1)}, f32[274,128]{1,0:T(8,128)S(1)}) custom-call(f32[2192,128]{1,0:T(8,128)S(1)} %bitcast.9), custom_call_target="tpu_custom_call" | custom-call | flops 1000000 | bytes 1000000 | tf_op jit(solution)/shard_map/pallas_call | solution.py:286
  32.2 6.0 %collective-permute-start = (f32[274,128]{1,0:T(8,128)S(1)}, f32[274,128]{1,0:T(8,128)S(1)}, u32[]{:S(2)}, u32[]{:S(2)}) collective-permute-start(f32[274,128]{1,0:T(8,128)S(1)} %get-tuple-element.11), channel_id=1, source_target_pairs={{32,64},{64,32},{96,128},{128,96},{160,192},{192,160},{224,256},{2... | collective-permute-start | bytes 420872 | tf_op jit(solution)/shard_map/ppermute | solution.py:263
  38.2 2.4 %collective-permute-start.1 = (f32[274,128]{1,0:T(8,128)S(1)}, f32[274,128]{1,0:T(8,128)S(1)}, u32[]{:S(2)}, u32[]{:S(2)}) collective-permute-start(f32[274,128]{1,0:T(8,128)S(1)} %get-tuple-element.12), channel_id=1, source_target_pairs={{0,1},{1,0},{2,3},{3,2},{4,5},{5,4},{6,7},{7,6},{8,9},{9,8},{10,11... | collective-permute-start | bytes 420872 | tf_op jit(solution)/shard_map/ppermute | solution.py:263
  40.7 4.3 %collective-permute-start.2 = (f32[274,128]{1,0:T(8,128)S(1)}, f32[274,128]{1,0:T(8,128)S(1)}, u32[]{:S(2)}, u32[]{:S(2)}) collective-permute-start(f32[274,128]{1,0:T(8,128)S(1)} %get-tuple-element.13), channel_id=1, source_target_pairs={{1,2},{2,1},{3,4},{4,3},{5,6},{6,5},{7,8},{8,7},{9,10},{10,9},{11,... | collective-permute-start | bytes 420872 | tf_op jit(solution)/shard_map/ppermute | solution.py:263
  45.0 1.9 %collective-permute-start.3 = (f32[274,128]{1,0:T(8,128)S(1)}, f32[274,128]{1,0:T(8,128)S(1)}, u32[]{:S(2)}, u32[]{:S(2)}) collective-permute-start(f32[274,128]{1,0:T(8,128)S(1)} %get-tuple-element.14), channel_id=1, source_target_pairs={{0,32},{32,0},{64,96},{96,64},{128,160},{160,128},{192,224},{224,1... | collective-permute-start | bytes 420872 | tf_op jit(solution)/shard_map/ppermute | solution.py:263
  46.9 0.2 reshape.28.mix_ref
  47.1 0.0 collective-permute-done.lon2_ref
  47.2 1.1 %collective-permute-done.2.lat2_ref = f32[274,128]{1,0:T(8,128)S(1)} collective-permute-done((f32[274,128]{1,0:T(8,128)S(1)}, f32[274,128]{1,0:T(8,128)S(1)}, u32[]{:S(2)}, u32[]{:S(2)}) %collective-permute-start.2) | collective-permute-done | bytes 140320 | tf_op jit(solution)/shard_map/ppermute | solution.py:263
  48.3 0.0 copy-start.2
  48.3 1.1 %copy-done.2 = bf16[40,20,274]{2,0,1:T(8,128)(2,1)S(1)} copy-done((bf16[40,20,274]{2,0,1:T(8,128)(2,1)S(1)}, bf16[40,20,274]{2,0,1:T(8,128)(2,1)}, u32[]{:S(2)}) %copy-start.2) | copy-done | bytes 438424
  49.4 1.6 %shard_map.84 = (f32[800,128]{1,0:T(8,128)S(1)}, f32[8,128]{1,0:T(8,128)S(1)}) custom-call(f32[2192,128]{1,0:T(8,128)S(1)} %bitcast.10, f32[274,128]{1,0:T(8,128)S(1)} %collective-permute-done.lon2_ref, f32[274,128]{1,0:T(8,128)S(1)} %collective-permute-done.1.lat_ref, f32[274,128]{1,0:T(8,128)S(1)} %collective-permute-done.2.lat2_ref, ...), custom_call_target="tpu_custom_call" | custom-call | flops 1000000 | bytes 1000000 | tf_op jit(solution)/shard_map/pallas_call | solution.py:290
  51.0 2.6 %all-to-all-done.records_ref = f32[32,1,384]{2,1,0:T(1,128)S(1)} async-done(((f32[32,1,384]{2,1,0:T(1,128)}), f32[32,1,384]{2,1,0:T(1,128)S(1)}, u32[]{:S(2)}, u32[]{:S(2)}) %all-to-all-start) | async-done | bytes 49184 | tf_op jit(solution)/shard_map/all_to_all | solution.py:283
  53.6 0.2 shard_map.85.own_ref
  53.8 4.2 %collective-permute-start.7 = (f32[32,128]{1,0:T(8,128)S(1)}, f32[32,128]{1,0:T(8,128)S(1)}, u32[]{:S(2)}, u32[]{:S(2)}) collective-permute-start(f32[32,128]{1,0:T(8,128)S(1)} %shard_map.85.own_ref), channel_id=1, source_target_pairs={{32,64},{64,32},{96,128},{128,96},{160,192},{192,160},{224,256},{2... | collective-permute-start | bytes 49160 | tf_op jit(solution)/shard_map/ppermute | solution.py:263
  58.0 3.6 %collective-permute-start.6 = (f32[32,128]{1,0:T(8,128)S(1)}, f32[32,128]{1,0:T(8,128)S(1)}, u32[]{:S(2)}, u32[]{:S(2)}) collective-permute-start(f32[32,128]{1,0:T(8,128)S(1)} %shard_map.85.own_ref), channel_id=1, source_target_pairs={{0,1},{1,0},{2,3},{3,2},{4,5},{5,4},{6,7},{7,6},{8,9},{9,8},{10,11... | collective-permute-start | bytes 49160 | tf_op jit(solution)/shard_map/ppermute | solution.py:263
  61.6 2.2 %collective-permute-start.5 = (f32[32,128]{1,0:T(8,128)S(1)}, f32[32,128]{1,0:T(8,128)S(1)}, u32[]{:S(2)}, u32[]{:S(2)}) collective-permute-start(f32[32,128]{1,0:T(8,128)S(1)} %shard_map.85.own_ref), channel_id=1, source_target_pairs={{1,2},{2,1},{3,4},{4,3},{5,6},{6,5},{7,8},{8,7},{9,10},{10,9},{11,... | collective-permute-start | bytes 49160 | tf_op jit(solution)/shard_map/ppermute | solution.py:263
  63.8 1.9 %collective-permute-start.4 = (f32[32,128]{1,0:T(8,128)S(1)}, f32[32,128]{1,0:T(8,128)S(1)}, u32[]{:S(2)}, u32[]{:S(2)}) collective-permute-start(f32[32,128]{1,0:T(8,128)S(1)} %shard_map.85.own_ref), channel_id=1, source_target_pairs={{0,32},{32,0},{64,96},{96,64},{128,160},{160,128},{192,224},{224,1... | collective-permute-start | bytes 49160 | tf_op jit(solution)/shard_map/ppermute | solution.py:263
  65.8 0.3 copy.12
  66.1 1.2 %collective-permute-done.5.lat2_ref = f32[32,128]{1,0:T(8,128)S(1)} collective-permute-done((f32[32,128]{1,0:T(8,128)S(1)}, f32[32,128]{1,0:T(8,128)S(1)}, u32[]{:S(2)}, u32[]{:S(2)}) %collective-permute-start.5) | collective-permute-done | bytes 16416 | tf_op jit(solution)/shard_map/ppermute | solution.py:263
  67.2 1.9 %shard_map.86 = f32[2192,128]{1,0:T(8,128)} custom-call(f32[32,128]{1,0:T(8,128)S(1)} %shard_map.85.own_ref, f32[32,128]{1,0:T(8,128)S(1)} %collective-permute-done.4.lon_ref, f32[32,128]{1,0:T(8,128)S(1)} %collective-permute-done.5.lat2_ref, f32[32,128]{1,0:T(8,128)S(1)} %collective-permute-done.6.lat_ref, f32[32,128]{1,0:T(8,128)S(1)} %collective-permute-done.7.lon2_ref, ...), custom_call_target="tpu_custom_call" | custom-call | flops 1000000 | bytes 1000000 | tf_op jit(solution)/shard_map/pallas_call | solution.py:298
  (15 shorter events, 0.0 us)
Async XLA Ops:
  0.0 46.9 %copy-start.6 = (f32[2,137]{1,0:T(2,128)S(1)}, f32[2,137]{1,0:T(2,128)}, u32[]{:S(2)}) copy-start(f32[2,137]{1,0:T(2,128)} %param.9) | copy-start | bytes 3292
  0.0 48.3 %copy-start.5 = (s32[1,1,256]{2,1,0:T(1,128)S(1)}, s32[1,1,256]{2,1,0:T(1,128)}, u32[]{:S(2)}) copy-start(s32[1,1,256]{2,1,0:T(1,128)} %param.12) | copy-start | bytes 3076
  0.0 48.3 %copy-start.4 = (s32[8,128]{1,0:T(8,128)S(1)}, s32[8,128]{1,0:T(8,128)}, u32[]{:S(2)}) copy-start(s32[8,128]{1,0:T(8,128)} %mask_ref.1) | copy-start | bytes 12292
  1.6 52.0 %all-to-all-start = ((f32[32,1,384]{2,1,0:T(1,128)}), f32[32,1,384]{2,1,0:T(1,128)S(1)}, u32[]{:S(2)}, u32[]{:S(2)}) async-start(f32[32,1,384]{2,1,0:T(1,128)} %shard_map.82), calls=%async_computation | async-start | bytes 98304 | tf_op jit(solution)/shard_map/all_to_all | solution.py:283
  30.3 1.3 %copy-start = (f32[2,137,8,128]{3,2,1,0:T(8,128)S(1)}, f32[2,137,8,128]{3,2,1,0:T(8,128)}, u32[]{:S(2)}) copy-start(f32[2,137,8,128]{3,2,1,0:T(8,128)} %param.8) | copy-start | bytes 3366916
  31.5 16.7 %copy-start.1 = (f32[2,137,8,128]{3,2,1,0:T(8,128)S(1)}, f32[2,137,8,128]{3,2,1,0:T(8,128)}, u32[]{:S(2)}) copy-start(f32[2,137,8,128]{3,2,1,0:T(8,128)} %param.8) | copy-start | bytes 3366916
  32.2 14.9 %collective-permute-start = (f32[274,128]{1,0:T(8,128)S(1)}, f32[274,128]{1,0:T(8,128)S(1)}, u32[]{:S(2)}, u32[]{:S(2)}) collective-permute-start(f32[274,128]{1,0:T(8,128)S(1)} %get-tuple-element.11), channel_id=1, source_target_pairs={{32,64},{64,32},{96,128},{128,96},{160,192},{192,160},{224,256},{2... | collective-permute-start | bytes 420872 | tf_op jit(solution)/shard_map/ppermute | solution.py:263
  38.2 8.9 %collective-permute-start.1 = (f32[274,128]{1,0:T(8,128)S(1)}, f32[274,128]{1,0:T(8,128)S(1)}, u32[]{:S(2)}, u32[]{:S(2)}) collective-permute-start(f32[274,128]{1,0:T(8,128)S(1)} %get-tuple-element.12), channel_id=1, source_target_pairs={{0,1},{1,0},{2,3},{3,2},{4,5},{5,4},{6,7},{7,6},{8,9},{9,8},{10,11... | collective-permute-start | bytes 420872 | tf_op jit(solution)/shard_map/ppermute | solution.py:263
  40.7 7.6 %collective-permute-start.2 = (f32[274,128]{1,0:T(8,128)S(1)}, f32[274,128]{1,0:T(8,128)S(1)}, u32[]{:S(2)}, u32[]{:S(2)}) collective-permute-start(f32[274,128]{1,0:T(8,128)S(1)} %get-tuple-element.13), channel_id=1, source_target_pairs={{1,2},{2,1},{3,4},{4,3},{5,6},{6,5},{7,8},{8,7},{9,10},{10,9},{11,... | collective-permute-start | bytes 420872 | tf_op jit(solution)/shard_map/ppermute | solution.py:263
  45.0 3.3 %collective-permute-start.3 = (f32[274,128]{1,0:T(8,128)S(1)}, f32[274,128]{1,0:T(8,128)S(1)}, u32[]{:S(2)}, u32[]{:S(2)}) collective-permute-start(f32[274,128]{1,0:T(8,128)S(1)} %get-tuple-element.14), channel_id=1, source_target_pairs={{0,32},{32,0},{64,96},{96,64},{128,160},{160,128},{192,224},{224,1... | collective-permute-start | bytes 420872 | tf_op jit(solution)/shard_map/ppermute | solution.py:263
  48.3 1.1 %copy-start.2 = (bf16[40,20,274]{2,0,1:T(8,128)(2,1)S(1)}, bf16[40,20,274]{2,0,1:T(8,128)(2,1)}, u32[]{:S(2)}) copy-start(bf16[40,20,274]{2,0,1:T(8,128)(2,1)} %param.11) | copy-start | bytes 1315204
  49.3 16.4 %copy-start.3 = (bf16[40,20,274]{2,0,1:T(8,128)(2,1)S(1)}, bf16[40,20,274]{2,0,1:T(8,128)(2,1)}, u32[]{:S(2)}) copy-start(bf16[40,20,274]{2,0,1:T(8,128)(2,1)} %param.11) | copy-start | bytes 1315204
  53.8 12.2 %collective-permute-start.7 = (f32[32,128]{1,0:T(8,128)S(1)}, f32[32,128]{1,0:T(8,128)S(1)}, u32[]{:S(2)}, u32[]{:S(2)}) collective-permute-start(f32[32,128]{1,0:T(8,128)S(1)} %shard_map.85.own_ref), channel_id=1, source_target_pairs={{32,64},{64,32},{96,128},{128,96},{160,192},{192,160},{224,256},{2... | collective-permute-start | bytes 49160 | tf_op jit(solution)/shard_map/ppermute | solution.py:263
  58.0 8.1 %collective-permute-start.6 = (f32[32,128]{1,0:T(8,128)S(1)}, f32[32,128]{1,0:T(8,128)S(1)}, u32[]{:S(2)}, u32[]{:S(2)}) collective-permute-start(f32[32,128]{1,0:T(8,128)S(1)} %shard_map.85.own_ref), channel_id=1, source_target_pairs={{0,1},{1,0},{2,3},{3,2},{4,5},{5,4},{6,7},{7,6},{8,9},{9,8},{10,11... | collective-permute-start | bytes 49160 | tf_op jit(solution)/shard_map/ppermute | solution.py:263
  61.6 5.6 %collective-permute-start.5 = (f32[32,128]{1,0:T(8,128)S(1)}, f32[32,128]{1,0:T(8,128)S(1)}, u32[]{:S(2)}, u32[]{:S(2)}) collective-permute-start(f32[32,128]{1,0:T(8,128)S(1)} %shard_map.85.own_ref), channel_id=1, source_target_pairs={{1,2},{2,1},{3,4},{4,3},{5,6},{6,5},{7,8},{8,7},{9,10},{10,9},{11,... | collective-permute-start | bytes 49160 | tf_op jit(solution)/shard_map/ppermute | solution.py:263
  63.8 3.4 %collective-permute-start.4 = (f32[32,128]{1,0:T(8,128)S(1)}, f32[32,128]{1,0:T(8,128)S(1)}, u32[]{:S(2)}, u32[]{:S(2)}) collective-permute-start(f32[32,128]{1,0:T(8,128)S(1)} %shard_map.85.own_ref), channel_id=1, source_target_pairs={{0,32},{32,0},{64,96},{96,64},{128,160},{160,128},{192,224},{224,1... | collective-permute-start | bytes 49160 | tf_op jit(solution)/shard_map/ppermute | solution.py:263

commit v4 on v3

--- a/solution.py
+++ b/solution.py
@@ -12,7 +12,7 @@
 STRIDE = 48
 CH = 20
 NOWHERE = -1000000
-CHUNK = 96
+CHUNK = 112
 
 
 def iota(shape, dim):
@@ -78,11 +78,11 @@
         right = jnp.where(lane == r, pltpu.roll(row, r + 1, 1), right)
         left = jnp.where(lane == ROWS + r, pltpu.roll(row, ROWS + r, 1), left)
     even = is_even("lat")
-    lat_ref[...] = jnp.where(even, last, first)
-    lat2_ref[...] = jnp.where(even, first, last)
+    lat_ref[...] = jnp.where(even, last, first).astype(lat_ref.dtype)
+    lat2_ref[...] = jnp.where(even, first, last).astype(lat2_ref.dtype)
     even = is_even("lon")
-    lon_ref[...] = jnp.where(even, right, left)
-    lon2_ref[...] = jnp.where(even, left, right)
+    lon_ref[...] = jnp.where(even, right, left).astype(lon_ref.dtype)
+    lon2_ref[...] = jnp.where(even, left, right).astype(lon2_ref.dtype)
 
 
 def state_body(inc_ref, lon2_ref, lat_ref, lat2_ref, lon_ref, col_ref, mask_ref, mix_ref,
@@ -126,13 +126,14 @@
     near = ~plain
     meets = jnp.where(is_even("lat"), (ROWS - 1) * LANES, 0)
     chosen = jnp.where(near & (want == sub + meets), 1.0, 0.0).astype(jnp.bfloat16)
-    total = total + split_dot(lat_ref[...], chosen)
+    total = total + jnp.dot(lat_ref[...], chosen, preferred_element_type=jnp.float32)
     chosen = jnp.where(near & (want == sub + ((ROWS - 1) * LANES - meets)), 1.0, 0.0).astype(jnp.bfloat16)
-    total = total + split_dot(lat2_ref[...], chosen)
+    total = total + jnp.dot(lat2_ref[...], chosen, preferred_element_type=jnp.float32)
     on_left = (sub < ROWS) & (want == sub * LANES)
     on_right = (sub >= ROWS) & (sub < 2 * ROWS) & (want == (sub - ROWS) * LANES + LANES - 1)
     chosen = jnp.where(near & (on_left | on_right), 1.0, 0.0).astype(jnp.bfloat16)
-    total = total + split_dot(lon_ref[...] + lon2_ref[...], chosen)
+    sides = lon_ref[...].astype(jnp.float32) + lon2_ref[...].astype(jnp.float32)
+    total = total + jnp.dot(sides.astype(jnp.bfloat16), chosen, preferred_element_type=jnp.float32)
 
     state = total + mix_ref[...] * masked[0:1, :] * pltpu.roll(total, LANES - 32, 1)
     state = jnp.where(iota((depth, LANES), 1) < 32, state, 0.0).astype(jnp.bfloat16)
@@ -282,7 +283,7 @@
     )(obs.reshape(CH, 1, slots), obs_weight.reshape(CH, 1, slots), fp_class)
     records = lax.all_to_all(records, "lat", split_axis=0, concat_axis=0, tiled=True)
 
-    edge = struct((depth, LANES), f32)
+    edge = struct((depth, LANES), jnp.bfloat16)
     edges = call(edges_body, (edge, edge, edge, edge))(inc)
     swaps = (("lon", 1, True), ("lat", 0, False), ("lat", 1, False), ("lon", 0, True))
     edges = [swapped(x, *swap) for x, swap in zip(edges, swaps)]

time: 69.6 us -> 69.7 us (level)
  transfers between devices with their start and end apart: 9 -> 9, of which waited for: 3 -> 4; matrix products, arithmetic and copies ran while one was open for 1% -> 1% of each run, Pallas kernels for 3% -> 3%
where the time goes in v4:
time: 69.7 us; the launch traced here: 69.2 us
  starting transfers between devices  55.1 us (79%)
  Pallas kernels  5.79 us (8%)
  waiting for transfers between devices  5.38 us (8%)
  local copies, waits for them, and re-layouts  2.84 us (4%)
    all_to_all x1, starting transfers between devices, on_device(): lax.all_to_all(records, 'lat', split_axis=0, concat_axis=0, tiled=True)  28.6 us
    ppermute x8, starting transfers between devices, swapped(): return lax.ppermute(x, axis, pairs)  26.5 us
    all_to_all x1, waiting for transfers between devices, on_device(): lax.all_to_all(records, 'lat', split_axis=0, concat_axis=0, tiled=True)  3.09 us
    unnamed x14, local copies, waits for them, and re-layouts  2.33 us
    ppermute x8, waiting for transfers between devices, swapped(): return lax.ppermute(x, axis, pairs)  2.29 us
    pallas_call x1, Pallas kernels, on_device(): call(gradient_body, struct((depth * ROWS, LANES), f32), (pltpu.VMEM((kind...  1.86 us
    pallas_call x1, Pallas kernels, on_device(): call(records_body, struct((peers, 1, SLOT * STRIDE), f32), (pltpu.VMEM((L...  1.64 us
    pallas_call x1, Pallas kernels, on_device(): call(state_body, (struct((kinds, LANES), f32), struct((8, LANES), f32)),...  1.6 us
  transfers between devices with their start and end apart: 9, of which 4 were waited for; matrix products, arithmetic and copies ran while one was open for 1% of the time, Pallas kernels for 3%

profile of v4, /device:TPU:32, one launch (start us, length us, event | category | flops | bytes accessed | tf_op | source)
XLA Modules:
  0.0 69.2 jit_solution(9604582608444818445)
XLA Ops:
  0.0 1.6 %shard_map.82 = f32[32,1,384]{2,1,0:T(1,128)} custom-call(f32[20,1,256]{2,1,0:T(1,128)} %bitcast.16, f32[20,1,256]{2,1,0:T(1,128)} %bitcast.17, s32[1,1,256]{2,1,0:T(1,128)} %class_ref.1), custom_call_target="tpu_custom_call" | custom-call | flops 1000000 | bytes 1000000 | tf_op jit(solution)/shard_map/pallas_call | solution.py:279
  1.6 28.6 %all-to-all-start = ((f32[32,1,384]{2,1,0:T(1,128)}), f32[32,1,384]{2,1,0:T(1,128)S(1)}, u32[]{:S(2)}, u32[]{:S(2)}) async-start(f32[32,1,384]{2,1,0:T(1,128)} %shard_map.82), calls=%async_computation | async-start | bytes 98304 | tf_op jit(solution)/shard_map/all_to_all | solution.py:284
  30.3 0.0 copy-start
  30.3 1.2 %copy-done = f32[2,137,8,128]{3,2,1,0:T(8,128)S(1)} copy-done((f32[2,137,8,128]{3,2,1,0:T(8,128)S(1)}, f32[2,137,8,128]{3,2,1,0:T(8,128)}, u32[]{:S(2)}) %copy-start) | copy-done | bytes 1122328
  31.5 0.5 shard_map.83
  32.0 6.0 %collective-permute-start = (bf16[274,128]{1,0:T(8,128)(2,1)S(1)}, bf16[274,128]{1,0:T(8,128)(2,1)S(1)}, u32[]{:S(2)}, u32[]{:S(2)}) collective-permute-start(bf16[274,128]{1,0:T(8,128)(2,1)S(1)} %get-tuple-element.11), channel_id=1, source_target_pairs={{32,64},{64,32},{96,128},{128,96},{160,192},{192,160},{224,256},{2... | collective-permute-start | bytes 210440 | tf_op jit(solution)/shard_map/ppermute | solution.py:264
  38.0 2.4 %collective-permute-start.1 = (bf16[274,128]{1,0:T(8,128)(2,1)S(1)}, bf16[274,128]{1,0:T(8,128)(2,1)S(1)}, u32[]{:S(2)}, u32[]{:S(2)}) collective-permute-start(bf16[274,128]{1,0:T(8,128)(2,1)S(1)} %get-tuple-element.12), channel_id=1, source_target_pairs={{0,1},{1,0},{2,3},{3,2},{4,5},{5,4},{6,7},{7,6},{8,9},{9,8},{10,11... | collective-permute-start | bytes 210440 | tf_op jit(solution)/shard_map/ppermute | solution.py:264
  40.4 4.3 %collective-permute-start.2 = (bf16[274,128]{1,0:T(8,128)(2,1)S(1)}, bf16[274,128]{1,0:T(8,128)(2,1)S(1)}, u32[]{:S(2)}, u32[]{:S(2)}) collective-permute-start(bf16[274,128]{1,0:T(8,128)(2,1)S(1)} %get-tuple-element.13), channel_id=1, source_target_pairs={{1,2},{2,1},{3,4},{4,3},{5,6},{6,5},{7,8},{8,7},{9,10},{10,9},{11,... | collective-permute-start | bytes 210440 | tf_op jit(solution)/shard_map/ppermute | solution.py:264
  44.7 1.9 %collective-permute-start.3 = (bf16[274,128]{1,0:T(8,128)(2,1)S(1)}, bf16[274,128]{1,0:T(8,128)(2,1)S(1)}, u32[]{:S(2)}, u32[]{:S(2)}) collective-permute-start(bf16[274,128]{1,0:T(8,128)(2,1)S(1)} %get-tuple-element.14), channel_id=1, source_target_pairs={{0,32},{32,0},{64,96},{96,64},{128,160},{160,128},{192,224},{224,1... | collective-permute-start | bytes 210440 | tf_op jit(solution)/shard_map/ppermute | solution.py:264
  46.7 0.2 reshape.28.mix_ref
  46.9 0.3 collective-permute-done.2.lat2_ref
  47.2 0.7 %collective-permute-done.3.lon_ref = bf16[274,128]{1,0:T(8,128)(2,1)S(1)} collective-permute-done((bf16[274,128]{1,0:T(8,128)(2,1)S(1)}, bf16[274,128]{1,0:T(8,128)(2,1)S(1)}, u32[]{:S(2)}, u32[]{:S(2)}) %collective-permute-start.3) | collective-permute-done | bytes 70176 | tf_op jit(solution)/shard_map/ppermute | solution.py:264
  47.9 0.0 copy-start.2
  47.9 1.1 %copy-done.2 = bf16[40,20,274]{2,0,1:T(8,128)(2,1)S(1)} copy-done((bf16[40,20,274]{2,0,1:T(8,128)(2,1)S(1)}, bf16[40,20,274]{2,0,1:T(8,128)(2,1)}, u32[]{:S(2)}) %copy-start.2) | copy-done | bytes 438424
  49.0 1.6 %shard_map.84 = (f32[800,128]{1,0:T(8,128)S(1)}, f32[8,128]{1,0:T(8,128)S(1)}) custom-call(f32[2192,128]{1,0:T(8,128)S(1)} %bitcast.10, bf16[274,128]{1,0:T(8,128)(2,1)S(1)} %collective-permute-done.lon2_ref, bf16[274,128]{1,0:T(8,128)(2,1)S(1)} %collective-permute-done.1.lat_ref, bf16[274,128]{1,0:T(8,128)(2,1)S(1)} %collective-permute-done.2.lat2_ref, ...), custom_call_target="tpu_custom_call" | custom-call | flops 1000000 | bytes 1000000 | tf_op jit(solution)/shard_map/pallas_call | solution.py:291
  50.6 3.1 %all-to-all-done.records_ref = f32[32,1,384]{2,1,0:T(1,128)S(1)} async-done(((f32[32,1,384]{2,1,0:T(1,128)}), f32[32,1,384]{2,1,0:T(1,128)S(1)}, u32[]{:S(2)}, u32[]{:S(2)}) %all-to-all-start) | async-done | bytes 49184 | tf_op jit(solution)/shard_map/all_to_all | solution.py:284
  53.7 0.2 shard_map.85.own_ref
  53.9 4.1 %collective-permute-start.7 = (f32[32,128]{1,0:T(8,128)S(1)}, f32[32,128]{1,0:T(8,128)S(1)}, u32[]{:S(2)}, u32[]{:S(2)}) collective-permute-start(f32[32,128]{1,0:T(8,128)S(1)} %shard_map.85.own_ref), channel_id=1, source_target_pairs={{32,64},{64,32},{96,128},{128,96},{160,192},{192,160},{224,256},{2... | collective-permute-start | bytes 49160 | tf_op jit(solution)/shard_map/ppermute | solution.py:264
  58.1 3.7 %collective-permute-start.6 = (f32[32,128]{1,0:T(8,128)S(1)}, f32[32,128]{1,0:T(8,128)S(1)}, u32[]{:S(2)}, u32[]{:S(2)}) collective-permute-start(f32[32,128]{1,0:T(8,128)S(1)} %shard_map.85.own_ref), channel_id=1, source_target_pairs={{0,1},{1,0},{2,3},{3,2},{4,5},{5,4},{6,7},{7,6},{8,9},{9,8},{10,11... | collective-permute-start | bytes 49160 | tf_op jit(solution)/shard_map/ppermute | solution.py:264
  61.7 2.1 %collective-permute-start.5 = (f32[32,128]{1,0:T(8,128)S(1)}, f32[32,128]{1,0:T(8,128)S(1)}, u32[]{:S(2)}, u32[]{:S(2)}) collective-permute-start(f32[32,128]{1,0:T(8,128)S(1)} %shard_map.85.own_ref), channel_id=1, source_target_pairs={{1,2},{2,1},{3,4},{4,3},{5,6},{6,5},{7,8},{8,7},{9,10},{10,9},{11,... | collective-permute-start | bytes 49160 | tf_op jit(solution)/shard_map/ppermute | solution.py:264
  63.8 1.9 %collective-permute-start.4 = (f32[32,128]{1,0:T(8,128)S(1)}, f32[32,128]{1,0:T(8,128)S(1)}, u32[]{:S(2)}, u32[]{:S(2)}) collective-permute-start(f32[32,128]{1,0:T(8,128)S(1)} %shard_map.85.own_ref), channel_id=1, source_target_pairs={{0,32},{32,0},{64,96},{96,64},{128,160},{160,128},{192,224},{224,1... | collective-permute-start | bytes 49160 | tf_op jit(solution)/shard_map/ppermute | solution.py:264
  65.8 0.3 copy.12
  66.1 1.3 %collective-permute-done.5.lat2_ref = f32[32,128]{1,0:T(8,128)S(1)} collective-permute-done((f32[32,128]{1,0:T(8,128)S(1)}, f32[32,128]{1,0:T(8,128)S(1)}, u32[]{:S(2)}, u32[]{:S(2)}) %collective-permute-start.5) | collective-permute-done | bytes 16416 | tf_op jit(solution)/shard_map/ppermute | solution.py:264
  67.4 1.9 %shard_map.86 = f32[2192,128]{1,0:T(8,128)} custom-call(f32[32,128]{1,0:T(8,128)S(1)} %shard_map.85.own_ref, f32[32,128]{1,0:T(8,128)S(1)} %collective-permute-done.4.lon_ref, f32[32,128]{1,0:T(8,128)S(1)} %collective-permute-done.5.lat2_ref, f32[32,128]{1,0:T(8,128)S(1)} %collective-permute-done.6.lat_ref, f32[32,128]{1,0:T(8,128)S(1)} %collective-permute-done.7.lon2_ref, ...), custom_call_target="tpu_custom_call" | custom-call | flops 1000000 | bytes 1000000 | tf_op jit(solution)/shard_map/pallas_call | solution.py:299
  (15 shorter events, 0.0 us)
Async XLA Ops:
  0.0 46.7 %copy-start.6 = (f32[2,137]{1,0:T(2,128)S(1)}, f32[2,137]{1,0:T(2,128)}, u32[]{:S(2)}) copy-start(f32[2,137]{1,0:T(2,128)} %param.9) | copy-start | bytes 3292
  0.0 47.9 %copy-start.5 = (s32[1,1,256]{2,1,0:T(1,128)S(1)}, s32[1,1,256]{2,1,0:T(1,128)}, u32[]{:S(2)}) copy-start(s32[1,1,256]{2,1,0:T(1,128)} %param.12) | copy-start | bytes 3076
  0.0 47.9 %copy-start.4 = (s32[8,128]{1,0:T(8,128)S(1)}, s32[8,128]{1,0:T(8,128)}, u32[]{:S(2)}) copy-start(s32[8,128]{1,0:T(8,128)} %mask_ref.1) | copy-start | bytes 12292
  1.6 52.0 %all-to-all-start = ((f32[32,1,384]{2,1,0:T(1,128)}), f32[32,1,384]{2,1,0:T(1,128)S(1)}, u32[]{:S(2)}, u32[]{:S(2)}) async-start(f32[32,1,384]{2,1,0:T(1,128)} %shard_map.82), calls=%async_computation | async-start | bytes 98304 | tf_op jit(solution)/shard_map/all_to_all | solution.py:284
  30.3 1.3 %copy-start = (f32[2,137,8,128]{3,2,1,0:T(8,128)S(1)}, f32[2,137,8,128]{3,2,1,0:T(8,128)}, u32[]{:S(2)}) copy-start(f32[2,137,8,128]{3,2,1,0:T(8,128)} %param.8) | copy-start | bytes 3366916
  31.5 16.4 %copy-start.1 = (f32[2,137,8,128]{3,2,1,0:T(8,128)S(1)}, f32[2,137,8,128]{3,2,1,0:T(8,128)}, u32[]{:S(2)}) copy-start(f32[2,137,8,128]{3,2,1,0:T(8,128)} %param.8) | copy-start | bytes 3366916
  32.0 14.9 %collective-permute-start = (bf16[274,128]{1,0:T(8,128)(2,1)S(1)}, bf16[274,128]{1,0:T(8,128)(2,1)S(1)}, u32[]{:S(2)}, u32[]{:S(2)}) collective-permute-start(bf16[274,128]{1,0:T(8,128)(2,1)S(1)} %get-tuple-element.11), channel_id=1, source_target_pairs={{32,64},{64,32},{96,128},{128,96},{160,192},{192,160},{224,256},{2... | collective-permute-start | bytes 210440 | tf_op jit(solution)/shard_map/ppermute | solution.py:264
  38.0 8.9 %collective-permute-start.1 = (bf16[274,128]{1,0:T(8,128)(2,1)S(1)}, bf16[274,128]{1,0:T(8,128)(2,1)S(1)}, u32[]{:S(2)}, u32[]{:S(2)}) collective-permute-start(bf16[274,128]{1,0:T(8,128)(2,1)S(1)} %get-tuple-element.12), channel_id=1, source_target_pairs={{0,1},{1,0},{2,3},{3,2},{4,5},{5,4},{6,7},{7,6},{8,9},{9,8},{10,11... | collective-permute-start | bytes 210440 | tf_op jit(solution)/shard_map/ppermute | solution.py:264
  40.4 6.8 %collective-permute-start.2 = (bf16[274,128]{1,0:T(8,128)(2,1)S(1)}, bf16[274,128]{1,0:T(8,128)(2,1)S(1)}, u32[]{:S(2)}, u32[]{:S(2)}) collective-permute-start(bf16[274,128]{1,0:T(8,128)(2,1)S(1)} %get-tuple-element.13), channel_id=1, source_target_pairs={{1,2},{2,1},{3,4},{4,3},{5,6},{6,5},{7,8},{8,7},{9,10},{10,9},{11,... | collective-permute-start | bytes 210440 | tf_op jit(solution)/shard_map/ppermute | solution.py:264
  44.7 3.2 %collective-permute-start.3 = (bf16[274,128]{1,0:T(8,128)(2,1)S(1)}, bf16[274,128]{1,0:T(8,128)(2,1)S(1)}, u32[]{:S(2)}, u32[]{:S(2)}) collective-permute-start(bf16[274,128]{1,0:T(8,128)(2,1)S(1)} %get-tuple-element.14), channel_id=1, source_target_pairs={{0,32},{32,0},{64,96},{96,64},{128,160},{160,128},{192,224},{224,1... | collective-permute-start | bytes 210440 | tf_op jit(solution)/shard_map/ppermute | solution.py:264
  47.9 1.1 %copy-start.2 = (bf16[40,20,274]{2,0,1:T(8,128)(2,1)S(1)}, bf16[40,20,274]{2,0,1:T(8,128)(2,1)}, u32[]{:S(2)}) copy-start(bf16[40,20,274]{2,0,1:T(8,128)(2,1)} %param.11) | copy-start | bytes 1315204
  49.0 16.8 %copy-start.3 = (bf16[40,20,274]{2,0,1:T(8,128)(2,1)S(1)}, bf16[40,20,274]{2,0,1:T(8,128)(2,1)}, u32[]{:S(2)}) copy-start(bf16[40,20,274]{2,0,1:T(8,128)(2,1)} %param.11) | copy-start | bytes 1315204
  53.9 12.2 %collective-permute-start.7 = (f32[32,128]{1,0:T(8,128)S(1)}, f32[32,128]{1,0:T(8,128)S(1)}, u32[]{:S(2)}, u32[]{:S(2)}) collective-permute-start(f32[32,128]{1,0:T(8,128)S(1)} %shard_map.85.own_ref), channel_id=1, source_target_pairs={{32,64},{64,32},{96,128},{128,96},{160,192},{192,160},{224,256},{2... | collective-permute-start | bytes 49160 | tf_op jit(solution)/shard_map/ppermute | solution.py:264
  58.1 8.0 %collective-permute-start.6 = (f32[32,128]{1,0:T(8,128)S(1)}, f32[32,128]{1,0:T(8,128)S(1)}, u32[]{:S(2)}, u32[]{:S(2)}) collective-permute-start(f32[32,128]{1,0:T(8,128)S(1)} %shard_map.85.own_ref), channel_id=1, source_target_pairs={{0,1},{1,0},{2,3},{3,2},{4,5},{5,4},{6,7},{7,6},{8,9},{9,8},{10,11... | collective-permute-start | bytes 49160 | tf_op jit(solution)/shard_map/ppermute | solution.py:264
  61.7 5.6 %collective-permute-start.5 = (f32[32,128]{1,0:T(8,128)S(1)}, f32[32,128]{1,0:T(8,128)S(1)}, u32[]{:S(2)}, u32[]{:S(2)}) collective-permute-start(f32[32,128]{1,0:T(8,128)S(1)} %shard_map.85.own_ref), channel_id=1, source_target_pairs={{1,2},{2,1},{3,4},{4,3},{5,6},{6,5},{7,8},{8,7},{9,10},{10,9},{11,... | collective-permute-start | bytes 49160 | tf_op jit(solution)/shard_map/ppermute | solution.py:264
  63.8 3.5 %collective-permute-start.4 = (f32[32,128]{1,0:T(8,128)S(1)}, f32[32,128]{1,0:T(8,128)S(1)}, u32[]{:S(2)}, u32[]{:S(2)}) collective-permute-start(f32[32,128]{1,0:T(8,128)S(1)} %shard_map.85.own_ref), channel_id=1, source_target_pairs={{0,32},{32,0},{64,96},{96,64},{128,160},{160,128},{192,224},{224,1... | collective-permute-start | bytes 49160 | tf_op jit(solution)/shard_map/ppermute | solution.py:264
